TPU v7x, 64 devices: a 2x2x8 block of a 4x4x8 slice. The times are simulated.
64 devices in a mesh: rep: 8 (over x, y, core), dp: 8 (over z).
Axes of the slice: x: 2, y: 2, z: 8, core: 2. Of those that a mesh axis runs over, the one named last changes fastest.
The devices are a block of a 4x4x8 slice.
Arguments:
- x: bfloat16 [64, 4096, 512], P(('rep', 'dp')), parts along dimension 0
- dy: bfloat16 [64, 4096, 512], P(('rep', 'dp')), parts along dimension 0
- w_gate: bfloat16 [2, 512, 1536], P(None, 'dp')
- w_up: bfloat16 [2, 512, 1536], P(None, 'dp')
- w_down: bfloat16 [2, 1536, 512], P(None, 'dp')
Outputs:
- output 1: bfloat16 [64, 4096, 512], P(('rep', 'dp')), parts along dimension 0
- output 2: bfloat16 [16, 512, 1536], P('rep', 'dp'), parts along dimension 0
- output 3: bfloat16 [16, 512, 1536], P('rep', 'dp'), parts along dimension 0
- output 4: bfloat16 [16, 1536, 512], P('rep', 'dp'), parts along dimension 0
There are 8 independent parts. A program takes and returns all parts, laid end to end along the dimension named above; an argument that names none is the same for every part.
All inputs are finite; a program needn't handle non-finite values.
Results may differ from a plain program's by a relative error of at most 0.018.
Values are sent between devices in bfloat16 or wider.
A program may use at most 768 MiB of HBM per device.

v0:
```python
import jax
import jax.numpy as jnp
from jax import lax

NAMES = ("w_gate", "w_up", "w_down")


def matmul(a, w):
    return jnp.dot(a, w, preferred_element_type=jnp.float32).astype(jnp.bfloat16)


def normed(h):
    wide = h.astype(jnp.float32)
    scale = lax.rsqrt(jnp.mean(wide**2, -1, keepdims=True) + 1e-6)
    return (wide * scale).astype(jnp.bfloat16)


def layer(h, w):
    a = normed(h)
    gate = jnp.dot(a, w["w_gate"], preferred_element_type=jnp.float32)
    up = jnp.dot(a, w["w_up"], preferred_element_type=jnp.float32)
    return h + matmul((jax.nn.silu(gate) * up).astype(jnp.bfloat16), w["w_down"])


def stack(weights, h):
    for number in range(weights["w_gate"].shape[0]):
        h = layer(h, {name: w[number] for name, w in weights.items()})
    return h


def solution(mesh):
    groups = mesh.shape["rep"]

    def step(x, dy, *weights):
        shape = x.shape
        x, dy = (t.reshape(groups, -1, *t.shape[1:]) for t in (x, dy))

        def of_a_group(x, dy):
            _, back = jax.vjp(stack, dict(zip(NAMES, weights, strict=True)), x)
            by_weights, by_x = back(dy)
            return (by_x, *(by_weights[name] for name in NAMES))

        by_x, *by_weights = jax.vmap(of_a_group)(x, dy)
        return (by_x.reshape(shape), *(t.reshape(-1, *t.shape[2:]) for t in by_weights))

    return step
```

profile of v0, /device:TPU:22, one launch (start us, length us, event | category | flops | bytes accessed | tf_op | source)
XLA Modules:
  0.0 753.3 jit_solution(13104802528075204921)
XLA Ops:
  24.4 6.5 copy
  38.0 11.8 %all-gather.29.cloned.1.call-done = bf16[1,512,1536]{2,1,0:T(8,128)(2,1)} async-done(((bf16[1,64,1536]{2,1,0:T(8,128)(2,1)}), bf16[1,512,1536]{2,1,0:T(8,128)(2,1)}) %all-gather.29.cloned.1.call-update) | async-done | bytes 1572880 | tf_op jit(solution)/vmap(jvp())/squeeze | solution.py:27
  49.8 13.9 %fusion.232 = f32[4096,1536]{1,0:T(8,128)} fusion(bf16[1,4096,512]{2,1,0:T(8,128)(2,1)} %param.13, f32[4096]{0:T(1024)S(1)} %get-tuple-element.267, bf16[1,512,1536]{2,1,0:T(8,128)(2,1)} %all-gather.29.cloned.1.call-done), kind=kOutput, calls=%fused_computation.252 | convolution fusion | flops 6448742400 | bytes 30949376 | tf_op jit(solution)/vmap(jvp())/dot_general | solution.py:20
  63.7 22.5 %all-gather.31.cloned.1.call-done = bf16[1,512,1536]{2,1,0:T(8,128)(2,1)} async-done(((bf16[1,64,1536]{2,1,0:T(8,128)(2,1)}), bf16[1,512,1536]{2,1,0:T(8,128)(2,1)}) %all-gather.31.cloned.1.call-update) | async-done | bytes 1572880 | tf_op jit(solution)/vmap(jvp())/squeeze | solution.py:27
  86.1 26.0 %fusion.168 = (bf16[1,1,4096,1536]{3,2,1,0:T(8,128)(2,1)}, f32[4096,1536]{1,0:T(8,128)}) fusion(f32[4096,1536]{1,0:T(8,128)} %fusion.232, bf16[1,512,1536]{2,1,0:T(8,128)(2,1)} %all-gather.31.cloned.1.call-done, bf16[1,4096,512]{2,1,0:T(8,128)(2,1)} %param.13, f32[4096]{0:T(1024)S(1)} %get-tuple-element.267), kind=kOutput, calls=%fused_computation.195 | convolution fusion | flops 6486491136 | bytes 68698112 | tf_op jit(solution)/vmap(jvp())/dot_general | solution.py:21
  112.1 15.6 %copy.4 = bf16[1,1,4096,1536]{2,3,1,0:T(8,128)(2,1)} copy(bf16[1,1,4096,1536]{3,2,1,0:T(8,128)(2,1)} %get-tuple-element.268) | data formatting | bytes 25165824
  127.7 11.3 %fusion.184 = (f32[4096]{0:T(1024)S(1)}, bf16[1,1,4096,512]{2,3,1,0:T(8,128)(2,1)S(1)}) fusion(bf16[1,1536,512]{2,1,0:T(8,128)(2,1)} %all-gather.33.cloned.1.call-done, bf16[1,1,4096,1536]{3,2,1,0:T(8,128)(2,1)} %get-tuple-element.268, bf16[1,4096,512]{1,2,0:T(8,128)(2,1)} %copy.1), kind=kOutput, calls=%fused_computation.227 | convolution fusion | flops 6452932608 | bytes 22560768 | tf_op jit(solution)/vmap(jvp())/dot_general | solution.py:9
  143.8 14.9 %all-gather.37.cloned.1.call-done = bf16[1,1536,512]{2,1,0:T(8,128)(2,1)} async-done(((bf16[1,192,512]{2,1,0:T(8,128)(2,1)}), bf16[1,1536,512]{2,1,0:T(8,128)(2,1)}) %all-gather.37.cloned.1.call-update) | async-done | bytes 1572880 | tf_op jit(solution)/vmap(jvp())/squeeze | solution.py:27
  158.7 12.3 %fusion.172 = bf16[1,1,4096,1536]{3,2,1,0:T(8,128)(2,1)} fusion(bf16[1,4096,512]{2,1,0:T(8,128)(2,1)} %param.12, bf16[1,1536,512]{2,1,0:T(8,128)(2,1)} %all-gather.37.cloned.1.call-done), kind=kOutput, calls=%fused_computation.208 | convolution fusion | flops 6448742400 | bytes 18350080 | tf_op jit(solution)/vmap(transpose(jvp()))/dot_general | solution.py:9
  171.0 23.9 %all-gather.39.cloned.1.call-done = bf16[1,512,1536]{2,1,0:T(8,128)(2,1)} async-done(((bf16[1,64,1536]{2,1,0:T(8,128)(2,1)}), bf16[1,512,1536]{2,1,0:T(8,128)(2,1)}) %all-gather.39.cloned.1.call-update) | async-done | bytes 1572880 | tf_op jit(solution)/vmap(jvp())/squeeze | solution.py:27
  194.9 13.9 %fusion.226 = f32[4096,1536]{1,0:T(8,128)} fusion(bf16[1,1,4096,512]{2,3,1,0:T(8,128)(2,1)} %fusion.185, bf16[1,512,1536]{2,1,0:T(8,128)(2,1)} %all-gather.39.cloned.1.call-done), kind=kOutput, calls=%fused_computation.247 | convolution fusion | flops 6442450944 | bytes 30932992 | tf_op jit(solution)/vmap(jvp())/dot_general | solution.py:21
  208.8 22.4 %all-gather.35.cloned.1.call-done = bf16[1,512,1536]{2,1,0:T(8,128)(2,1)} async-done(((bf16[1,64,1536]{2,1,0:T(8,128)(2,1)}), bf16[1,512,1536]{2,1,0:T(8,128)(2,1)}) %all-gather.35.cloned.1.call-update) | async-done | bytes 1572880 | tf_op jit(solution)/vmap(jvp())/squeeze | solution.py:27
  231.1 35.7 %fusion.153 = (bf16[1,1,4096,1536]{3,2,1,0:T(8,128)(2,1)}, bf16[1,1,4096,1536]{3,2,1,0:T(8,128)(2,1)}, f32[4096,1536]{1,0:T(8,128)}) fusion(f32[4096,1536]{1,0:T(8,128)} %fusion.226, bf16[1,1,4096,1536]{3,2,1,0:T(8,128)(2,1)} %fusion.172, bf16[1,512,1536]{2,1,0:T(8,128)(2,1)} %all-gather.35.cloned.1.call-done, bf16[1,1,4096,512]{2,3,1,0:T(8,128)(2,1)} %fusion.185), kind=kOutput, calls=%fused_computation.175 | convolution fusion | flops 6536822784 | bytes 93847552 | tf_op jit(solution)/vmap(jvp())/dot_general | solution.py:20
  266.8 32.6 %fusion.162 = bf16[1,1,4096,1536]{3,2,1,0:T(8,128)(2,1)} fusion(f32[4096,1536]{1,0:T(8,128)} %fusion.226, f32[4096,1536]{1,0:T(8,128)} %get-tuple-element.272), kind=kLoop, calls=%fused_computation.185 | loop fusion | flops 37748736 | bytes 62914560 | tf_op jit(solution)/vmap(jvp())/convert_element_type | solution.py:22
  299.4 15.9 %copy.2 = bf16[1,1,4096,1536]{2,3,1,0:T(8,128)(2,1)} copy(bf16[1,1,4096,1536]{3,2,1,0:T(8,128)(2,1)} %fusion.162) | data formatting | bytes 25165824
  315.3 48.7 %while.16 = (bf16[1,1,4096,1536]{2,3,1,0:T(8,128)(2,1)}, bf16[1,1,4096,512]{3,2,1,0:T(8,128)(2,1)}, f32[1,192,512]{2,1,0:T(8,128)S(1)}, f32[1,192,512]{2,1,0:T(8...) while((bf16[1,1,4096,1536]{2,3,1,0:T(8,128)(2,1)}, ...), condition=%wide.windowed_dot_general_cond_rs.4.clone, body=%wide.windowed_dot_general_body_rs.4.clone.sunk | while | flops 3234398208 | bytes 114819744 | solution.py:9
  356.1 6.9 collective-permute-done.18
  363.9 9.9 %fusion.190 = bf16[4096,512]{0,1:T(8,128)(2,1)S(1)} fusion(bf16[1,1,4096,1536]{3,2,1,0:T(8,128)(2,1)} %get-tuple-element.628, bf16[1,512,1536]{2,1,0:T(8,128)(2,1)S(1)} %copy-done.32), kind=kOutput, calls=%fused_computation.231 | convolution fusion | flops 6442450944 | bytes 18350080 | tf_op jit(solution)/vmap(transpose(jvp()))/dot_general | solution.py:21
  373.9 10.4 %fusion.186 = (f32[4096]{0:T(1024)S(1)}, bf16[1,1,4096,512]{2,3,1,0:T(8,128)(2,1)S(1)}) fusion(bf16[1,1,4096,512]{2,3,1,0:T(8,128)(2,1)S(1)} %copy-done.8, bf16[4096,512]{0,1:T(8,128)(2,1)S(1)} %fusion.190, bf16[1,512,1536]{2,1,0:T(8,128)(2,1)S(1)} %copy-done.33, bf16[1,1,4096,1536]{3,2,1,0:T(8,128)(2,1)} %get-tuple-element.550), kind=kOutput, calls=%fused_computation.229 | convolution fusion | flops 6452932608 | bytes 26755072 | tf_op jit(solution)/vmap(transpose(jvp()))/dot_general | solution.py:20
  388.7 6.5 copy.5
  395.2 53.5 %while.17 = (bf16[1,1,4096,1536]{2,3,1,0:T(8,128)(2,1)}, bf16[1,1,4096,512]{3,2,1,0:T(8,128)(2,1)}, f32[1,192,512]{2,1,0:T(8,128)S(1)}, f32[1,192,512]{2,1,0:T(8...) while((bf16[1,1,4096,1536]{2,3,1,0:T(8,128)(2,1)}, ...), condition=%wide.windowed_dot_general_cond_rs.5.clone, body=%wide.windowed_dot_general_body_rs.5.clone.sunk | while | flops 3234398208 | bytes 114819744 | solution.py:9
  413.0 8.1 %collective-permute-done.22 = f32[1,192,512]{2,1,0:T(8,128)S(1)} collective-permute-done((f32[1,192,512]{2,1,0:T(8,128)S(1)}, f32[1,192,512]{2,1,0:T(8,128)S(1)}, u32[]{:S(2)}, u32[]{:S(2)}) %collective-permute-start.22) | collective-permute-done | bytes 393248 | tf_op jit(solution)/vmap(transpose(jvp()))/dot_general | solution.py:9
  439.6 8.2 %collective-permute-done.22 = f32[1,192,512]{2,1,0:T(8,128)S(1)} collective-permute-done((f32[1,192,512]{2,1,0:T(8,128)S(1)}, f32[1,192,512]{2,1,0:T(8,128)S(1)}, u32[]{:S(2)}, u32[]{:S(2)}) %collective-permute-start.22) | collective-permute-done | bytes 393248 | tf_op jit(solution)/vmap(transpose(jvp()))/dot_general | solution.py:9
  449.5 51.7 %while.14 = (bf16[1,1,4096,512]{2,3,1,0:T(8,128)(2,1)}, bf16[1,1,4096,1536]{3,2,1,0:T(8,128)(2,1)}, f32[1,64,1536]{2,1,0:T(8,128)S(1)}, f32[1,64,1536]{2,1,0:T(8...) while((bf16[1,1,4096,512]{2,3,1,0:T(8,128)(2,1)}, ...), condition=%wide.windowed_dot_general_cond_rs.2.clone, body=%wide.windowed_dot_general_body_rs.2.clone.sunk | while | flops 3226009600 | bytes 47710820 | solution.py:21
  455.3 6.7 fusion.323
  468.8 6.7 fusion.325
  482.8 6.7 fusion.323
  493.6 6.7 fusion.325
  501.2 31.8 %fusion.155 = (bf16[1,1,4096,1536]{3,2,1,0:T(8,128)(2,1)}, bf16[1,1,4096,1536]{3,2,1,0:T(8,128)(2,1)}) fusion(f32[4096,1536]{1,0:T(8,128)} %fusion.232, f32[4096,1536]{1,0:T(8,128)} %get-tuple-element.269, bf16[1,1536,512]{2,1,0:T(8,128)(2,1)} %all-gather.33.cloned.1.call-done, bf16[1,1,4096,512]{2,3,1,0:T(8,128)(2,1)} %fusion.222), kind=kOutput, calls=%fused_computation.177 | convolution fusion | flops 6543114240 | bytes 81264640 | tf_op jit(solution)/vmap(transpose(jvp()))/dot_general | solution.py:9
  533.0 13.0 %fusion.196 = bf16[4096,512]{0,1:T(8,128)(2,1)} fusion(bf16[1,1,4096,1536]{3,2,1,0:T(8,128)(2,1)} %get-tuple-element.589, bf16[1,512,1536]{2,1,0:T(8,128)(2,1)S(1)} %copy-done.31), kind=kOutput, calls=%fused_computation.233 | convolution fusion | flops 6442450944 | bytes 18350080 | tf_op jit(solution)/vmap(transpose(jvp()))/dot_general | solution.py:21
  546.0 12.1 %fusion.183 = (bf16[1,1,4096,512]{2,3,1,0:T(8,128)(2,1)}, f32[4096]{0:T(1024)}, bf16[1,1,4096,512]{2,3,1,0:T(8,128)(2,1)}) fusion(bf16[1,4096,512]{1,2,0:T(8,128)(2,1)S(1)} %copy-done.6, f32[4096]{0:T(1024)S(1)} %bitcast.593, bf16[4096,512]{0,1:T(8,128)(2,1)} %fusion.196, bf16[1,512,1536]{2,1,0:T(8,128)(2,1)} %all-gather.29.cloned.1.call-done, ...), kind=kOutput, calls=%fused_computation.226 | convolution fusion | flops 6457126912 | bytes 30965760 | tf_op jit(solution)/vmap(transpose(jvp()))/dot_general | solution.py:20
  558.1 46.3 %while.15 = (bf16[1,1,4096,512]{2,3,1,0:T(8,128)(2,1)}, bf16[1,1,4096,1536]{3,2,1,0:T(8,128)(2,1)}, f32[1,64,1536]{2,1,0:T(8,128)S(1)}, f32[1,64,1536]{2,1,0:T(8...) while((bf16[1,1,4096,512]{2,3,1,0:T(8,128)(2,1)}, ...), condition=%wide.windowed_dot_general_cond_rs.3.clone, body=%wide.windowed_dot_general_body_rs.3.clone.sunk | while | flops 3226009600 | bytes 47710820 | solution.py:21
  563.7 6.7 fusion.331
  574.5 6.7 fusion.333
  586.7 6.7 fusion.331
  597.6 6.7 fusion.333
  605.2 57.7 %while.12 = (bf16[1,1,4096,512]{2,3,1,0:T(8,128)(2,1)}, bf16[1,1,4096,1536]{3,2,1,0:T(8,128)(2,1)}, f32[1,64,1536]{2,1,0:T(8,128)S(1)}, f32[1,64,1536]{2,1,0:T(8...) while((bf16[1,1,4096,512]{2,3,1,0:T(8,128)(2,1)}, ...), condition=%wide.windowed_dot_general_cond_rs.clone, body=%wide.windowed_dot_general_body_rs.clone.sunk | while | flops 3226009600 | bytes 47710820 | solution.py:20
  613.1 6.7 fusion.307
  626.0 6.7 fusion.309
  643.2 6.7 fusion.307
  654.0 6.7 fusion.309
  663.4 53.9 %while.13 = (bf16[1,1,4096,512]{2,3,1,0:T(8,128)(2,1)}, bf16[1,1,4096,1536]{3,2,1,0:T(8,128)(2,1)}, f32[1,64,1536]{2,1,0:T(8,128)S(1)}, f32[1,64,1536]{2,1,0:T(8...) while((bf16[1,1,4096,512]{2,3,1,0:T(8,128)(2,1)}, ...), condition=%wide.windowed_dot_general_cond_rs.1.clone, body=%wide.windowed_dot_general_body_rs.1.clone.sunk | while | flops 3226009600 | bytes 47710820 | solution.py:20
  669.8 6.7 fusion.315
  680.7 6.7 fusion.317
  695.6 6.7 fusion.315
  706.5 6.7 fusion.317
  718.1 7.5 fusion.221
  725.6 6.5 copy.6
  (301 shorter events, 205.8 us)
Async XLA Ops:
  7.2 42.6 %all-gather.29.cloned.1.call-start = ((), (), s32[]{:S(2)}) async-start(), calls=%async_computation | async-start | bytes 1769472 | tf_op jit(solution)/vmap(jvp())/squeeze | solution.py:27
  9.1 77.0 %all-gather.31.cloned.1.call-start = ((), (), s32[]{:S(2)}) async-start(), calls=%async_computation.1 | async-start | bytes 1769472 | tf_op jit(solution)/vmap(jvp())/squeeze | solution.py:27
  11.0 116.6 %all-gather.33.cloned.1.call-start = ((), (), s32[]{:S(2)}) async-start(), calls=%async_computation.2 | async-start | bytes 1769472 | tf_op jit(solution)/vmap(jvp())/squeeze | solution.py:27
  13.0 145.8 %all-gather.37.cloned.1.call-start = ((), (), s32[]{:S(2)}) async-start(), calls=%async_computation.4 | async-start | bytes 1769472 | tf_op jit(solution)/vmap(jvp())/squeeze | solution.py:27
  13.6 181.3 %all-gather.39.cloned.1.call-start = ((), (), s32[]{:S(2)}) async-start(), calls=%async_computation.5 | async-start | bytes 1769472 | tf_op jit(solution)/vmap(jvp())/squeeze | solution.py:27
  14.2 216.9 %all-gather.35.cloned.1.call-start = ((), (), s32[]{:S(2)}) async-start(), calls=%async_computation.3 | async-start | bytes 1769472 | tf_op jit(solution)/vmap(jvp())/squeeze | solution.py:27
  315.3 11.1 %collective-permute-start.16 = (f32[1,192,512]{2,1,0:T(8,128)S(1)}, f32[1,192,512]{2,1,0:T(8,128)S(1)}, u32[]{:S(2)}, u32[]{:S(2)}) collective-permute-start(f32[1,192,512]{2,1,0:T(8,128)S(1)} %broadcast_select_fusion.32), channel_id=38, source_target_pairs={{0,1},{1,2},{2,3},{3,4},{4,5},{5,6},{6,7},{7,0},{8,9},{9,10},{10,1... | collective-permute-start | bytes 1179656 | tf_op jit(solution)/vmap(transpose(jvp()))/dot_general | solution.py:9
  338.5 11.6 %collective-permute-start.16 = (f32[1,192,512]{2,1,0:T(8,128)S(1)}, f32[1,192,512]{2,1,0:T(8,128)S(1)}, u32[]{:S(2)}, u32[]{:S(2)}) collective-permute-start(f32[1,192,512]{2,1,0:T(8,128)S(1)} %broadcast_select_fusion.32), channel_id=38, source_target_pairs={{0,1},{1,2},{2,3},{3,4},{4,5},{5,6},{6,7},{7,0},{8,9},{9,10},{10,1... | collective-permute-start | bytes 1179656 | tf_op jit(solution)/vmap(transpose(jvp()))/dot_general | solution.py:9
  338.7 11.6 %collective-permute-start.17 = (f32[1,192,512]{2,1,0:T(8,128)S(1)}, f32[1,192,512]{2,1,0:T(8,128)S(1)}, u32[]{:S(2)}, u32[]{:S(2)}) collective-permute-start(f32[1,192,512]{2,1,0:T(8,128)S(1)} %broadcast_select_fusion.33), channel_id=37, source_target_pairs={{0,7},{1,0},{2,1},{3,2},{4,3},{5,4},{6,5},{7,6},{8,15},{9,8},{10,9... | collective-permute-start | bytes 1179656 | tf_op jit(solution)/vmap(transpose(jvp()))/dot_general | solution.py:9
  350.4 12.6 %collective-permute-start.18 = (f32[1,192,512]{2,1,0:T(8,128)S(1)}, f32[1,192,512]{2,1,0:T(8,128)S(1)}, u32[]{:S(2)}, u32[]{:S(2)}) collective-permute-start(f32[1,192,512]{2,1,0:T(8,128)S(1)} %get-tuple-element.497), channel_id=40, source_target_pairs={{0,1},{1,2},{2,3},{3,4},{4,5},{5,6},{6,7},{7,0},{8,9},{9,10},{10,1... | collective-permute-start | bytes 1179656 | tf_op jit(solution)/vmap(transpose(jvp()))/dot_general | solution.py:9
  351.7 11.3 %collective-permute-start.19 = (f32[1,192,512]{2,1,0:T(8,128)S(1)}, f32[1,192,512]{2,1,0:T(8,128)S(1)}, u32[]{:S(2)}, u32[]{:S(2)}) collective-permute-start(f32[1,192,512]{2,1,0:T(8,128)S(1)} %get-tuple-element.498), channel_id=39, source_target_pairs={{0,7},{1,0},{2,1},{3,2},{4,3},{5,4},{6,5},{7,6},{8,15},{9,8},{10,9... | collective-permute-start | bytes 1179656 | tf_op jit(solution)/vmap(transpose(jvp()))/dot_general | solution.py:9
  363.9 369.7 %collective-permute-start.28 = (f32[1,192,512]{2,1,0:T(8,128)}, f32[1,192,512]{2,1,0:T(8,128)}, u32[]{:S(2)}, u32[]{:S(2)}) collective-permute-start(f32[1,192,512]{2,1,0:T(8,128)} %get-tuple-element.45), channel_id=41, source_target_pairs={{0,1},{1,2},{2,3},{3,4},{4,5},{5,6},{6,7},{7,0},{8,9},{9,10},{10,1... | collective-permute-start | bytes 1179656 | tf_op jit(solution)/vmap(transpose(jvp()))/dot_general | solution.py:9
  395.2 12.4 %collective-permute-start.20 = (f32[1,192,512]{2,1,0:T(8,128)S(1)}, f32[1,192,512]{2,1,0:T(8,128)S(1)}, u32[]{:S(2)}, u32[]{:S(2)}) collective-permute-start(f32[1,192,512]{2,1,0:T(8,128)S(1)} %broadcast_select_fusion.34), channel_id=44, source_target_pairs={{0,1},{1,2},{2,3},{3,4},{4,5},{5,6},{6,7},{7,0},{8,9},{9,10},{10,1... | collective-permute-start | bytes 1179656 | tf_op jit(solution)/vmap(transpose(jvp()))/dot_general | solution.py:9
  407.8 13.2 %collective-permute-start.22 = (f32[1,192,512]{2,1,0:T(8,128)S(1)}, f32[1,192,512]{2,1,0:T(8,128)S(1)}, u32[]{:S(2)}, u32[]{:S(2)}) collective-permute-start(f32[1,192,512]{2,1,0:T(8,128)S(1)} %get-tuple-element.506), channel_id=46, source_target_pairs={{0,1},{1,2},{2,3},{3,4},{4,5},{5,6},{6,7},{7,0},{8,9},{9,10},{10,1... | collective-permute-start | bytes 1179656 | tf_op jit(solution)/vmap(transpose(jvp()))/dot_general | solution.py:9
  408.4 12.6 %collective-permute-start.23 = (f32[1,192,512]{2,1,0:T(8,128)S(1)}, f32[1,192,512]{2,1,0:T(8,128)S(1)}, u32[]{:S(2)}, u32[]{:S(2)}) collective-permute-start(f32[1,192,512]{2,1,0:T(8,128)S(1)} %get-tuple-element.507), channel_id=45, source_target_pairs={{0,7},{1,0},{2,1},{3,2},{4,3},{5,4},{6,5},{7,6},{8,15},{9,8},{10,9... | collective-permute-start | bytes 1179656 | tf_op jit(solution)/vmap(transpose(jvp()))/dot_general | solution.py:9
  423.0 11.3 %collective-permute-start.20 = (f32[1,192,512]{2,1,0:T(8,128)S(1)}, f32[1,192,512]{2,1,0:T(8,128)S(1)}, u32[]{:S(2)}, u32[]{:S(2)}) collective-permute-start(f32[1,192,512]{2,1,0:T(8,128)S(1)} %broadcast_select_fusion.34), channel_id=44, source_target_pairs={{0,1},{1,2},{2,3},{3,4},{4,5},{5,6},{6,7},{7,0},{8,9},{9,10},{10,1... | collective-permute-start | bytes 1179656 | tf_op jit(solution)/vmap(transpose(jvp()))/dot_general | solution.py:9
  423.6 10.7 %collective-permute-start.21 = (f32[1,192,512]{2,1,0:T(8,128)S(1)}, f32[1,192,512]{2,1,0:T(8,128)S(1)}, u32[]{:S(2)}, u32[]{:S(2)}) collective-permute-start(f32[1,192,512]{2,1,0:T(8,128)S(1)} %broadcast_select_fusion.35), channel_id=43, source_target_pairs={{0,7},{1,0},{2,1},{3,2},{4,3},{5,4},{6,5},{7,6},{8,15},{9,8},{10,9... | collective-permute-start | bytes 1179656 | tf_op jit(solution)/vmap(transpose(jvp()))/dot_general | solution.py:9
  434.5 13.3 %collective-permute-start.22 = (f32[1,192,512]{2,1,0:T(8,128)S(1)}, f32[1,192,512]{2,1,0:T(8,128)S(1)}, u32[]{:S(2)}, u32[]{:S(2)}) collective-permute-start(f32[1,192,512]{2,1,0:T(8,128)S(1)} %get-tuple-element.506), channel_id=46, source_target_pairs={{0,1},{1,2},{2,3},{3,4},{4,5},{5,6},{6,7},{7,0},{8,9},{9,10},{10,1... | collective-permute-start | bytes 1179656 | tf_op jit(solution)/vmap(transpose(jvp()))/dot_general | solution.py:9
  434.6 13.2 %collective-permute-start.23 = (f32[1,192,512]{2,1,0:T(8,128)S(1)}, f32[1,192,512]{2,1,0:T(8,128)S(1)}, u32[]{:S(2)}, u32[]{:S(2)}) collective-permute-start(f32[1,192,512]{2,1,0:T(8,128)S(1)} %get-tuple-element.507), channel_id=45, source_target_pairs={{0,7},{1,0},{2,1},{3,2},{4,3},{5,4},{6,5},{7,6},{8,15},{9,8},{10,9... | collective-permute-start | bytes 1179656 | tf_op jit(solution)/vmap(transpose(jvp()))/dot_general | solution.py:9
  448.7 289.1 %collective-permute-start.29 = (f32[1,192,512]{2,1,0:T(8,128)}, f32[1,192,512]{2,1,0:T(8,128)}, u32[]{:S(2)}, u32[]{:S(2)}) collective-permute-start(f32[1,192,512]{2,1,0:T(8,128)} %get-tuple-element.47), channel_id=47, source_target_pairs={{0,1},{1,2},{2,3},{3,4},{4,5},{5,6},{6,7},{7,0},{8,9},{9,10},{10,1... | collective-permute-start | bytes 1179656 | tf_op jit(solution)/vmap(transpose(jvp()))/dot_general | solution.py:9
  449.9 15.5 %collective-permute-start.8 = (f32[1,64,1536]{2,1,0:T(8,128)S(1)}, f32[1,64,1536]{2,1,0:T(8,128)S(1)}, u32[]{:S(2)}, u32[]{:S(2)}) collective-permute-start(f32[1,64,1536]{2,1,0:T(8,128)S(1)} %broadcast_select_fusion.28), channel_id=26, source_target_pairs={{0,1},{1,2},{2,3},{3,4},{4,5},{5,6},{6,7},{7,0},{8,9},{9,10},{10,1... | collective-permute-start | bytes 1179656 | tf_op jit(solution)/vmap(transpose(jvp()))/dot_general | solution.py:21
  450.1 15.3 %collective-permute-start.9 = (f32[1,64,1536]{2,1,0:T(8,128)S(1)}, f32[1,64,1536]{2,1,0:T(8,128)S(1)}, u32[]{:S(2)}, u32[]{:S(2)}) collective-permute-start(f32[1,64,1536]{2,1,0:T(8,128)S(1)} %broadcast_select_fusion.29), channel_id=25, source_target_pairs={{0,7},{1,0},{2,1},{3,2},{4,3},{5,4},{6,5},{7,6},{8,15},{9,8},{10,9... | collective-permute-start | bytes 1179656 | tf_op jit(solution)/vmap(transpose(jvp()))/dot_general | solution.py:21
  465.5 10.1 %collective-permute-start.10 = (f32[1,64,1536]{2,1,0:T(8,128)S(1)}, f32[1,64,1536]{2,1,0:T(8,128)S(1)}, u32[]{:S(2)}, u32[]{:S(2)}) collective-permute-start(f32[1,64,1536]{2,1,0:T(8,128)S(1)} %get-tuple-element.479), channel_id=28, source_target_pairs={{0,1},{1,2},{2,3},{3,4},{4,5},{5,6},{6,7},{7,0},{8,9},{9,10},{10,1... | collective-permute-start | bytes 1179656 | tf_op jit(solution)/vmap(transpose(jvp()))/dot_general | solution.py:21
  477.4 12.7 %collective-permute-start.8 = (f32[1,64,1536]{2,1,0:T(8,128)S(1)}, f32[1,64,1536]{2,1,0:T(8,128)S(1)}, u32[]{:S(2)}, u32[]{:S(2)}) collective-permute-start(f32[1,64,1536]{2,1,0:T(8,128)S(1)} %broadcast_select_fusion.28), channel_id=26, source_target_pairs={{0,1},{1,2},{2,3},{3,4},{4,5},{5,6},{6,7},{7,0},{8,9},{9,10},{10,1... | collective-permute-start | bytes 1179656 | tf_op jit(solution)/vmap(transpose(jvp()))/dot_general | solution.py:21
  477.6 12.6 %collective-permute-start.9 = (f32[1,64,1536]{2,1,0:T(8,128)S(1)}, f32[1,64,1536]{2,1,0:T(8,128)S(1)}, u32[]{:S(2)}, u32[]{:S(2)}) collective-permute-start(f32[1,64,1536]{2,1,0:T(8,128)S(1)} %broadcast_select_fusion.29), channel_id=25, source_target_pairs={{0,7},{1,0},{2,1},{3,2},{4,3},{5,4},{6,5},{7,6},{8,15},{9,8},{10,9... | collective-permute-start | bytes 1179656 | tf_op jit(solution)/vmap(transpose(jvp()))/dot_general | solution.py:21
  501.2 235.5 %collective-permute-start.26 = (f32[1,64,1536]{2,1,0:T(8,128)}, f32[1,64,1536]{2,1,0:T(8,128)}, u32[]{:S(2)}, u32[]{:S(2)}) collective-permute-start(f32[1,64,1536]{2,1,0:T(8,128)} %get-tuple-element.41), channel_id=29, source_target_pairs={{0,1},{1,2},{2,3},{3,4},{4,5},{5,6},{6,7},{7,0},{8,9},{9,10},{10,1... | collective-permute-start | bytes 1179656 | tf_op jit(solution)/vmap(transpose(jvp()))/dot_general | solution.py:21
  558.3 12.7 %collective-permute-start.12 = (f32[1,64,1536]{2,1,0:T(8,128)S(1)}, f32[1,64,1536]{2,1,0:T(8,128)S(1)}, u32[]{:S(2)}, u32[]{:S(2)}) collective-permute-start(f32[1,64,1536]{2,1,0:T(8,128)S(1)} %broadcast_select_fusion.30), channel_id=32, source_target_pairs={{0,1},{1,2},{2,3},{3,4},{4,5},{5,6},{6,7},{7,0},{8,9},{9,10},{10,1... | collective-permute-start | bytes 1179656 | tf_op jit(solution)/vmap(transpose(jvp()))/dot_general | solution.py:21
  558.5 12.6 %collective-permute-start.13 = (f32[1,64,1536]{2,1,0:T(8,128)S(1)}, f32[1,64,1536]{2,1,0:T(8,128)S(1)}, u32[]{:S(2)}, u32[]{:S(2)}) collective-permute-start(f32[1,64,1536]{2,1,0:T(8,128)S(1)} %broadcast_select_fusion.31), channel_id=31, source_target_pairs={{0,7},{1,0},{2,1},{3,2},{4,3},{5,4},{6,5},{7,6},{8,15},{9,8},{10,9... | collective-permute-start | bytes 1179656 | tf_op jit(solution)/vmap(transpose(jvp()))/dot_general | solution.py:21
  581.4 12.7 %collective-permute-start.12 = (f32[1,64,1536]{2,1,0:T(8,128)S(1)}, f32[1,64,1536]{2,1,0:T(8,128)S(1)}, u32[]{:S(2)}, u32[]{:S(2)}) collective-permute-start(f32[1,64,1536]{2,1,0:T(8,128)S(1)} %broadcast_select_fusion.30), channel_id=32, source_target_pairs={{0,1},{1,2},{2,3},{3,4},{4,5},{5,6},{6,7},{7,0},{8,9},{9,10},{10,1... | collective-permute-start | bytes 1179656 | tf_op jit(solution)/vmap(transpose(jvp()))/dot_general | solution.py:21
  581.6 12.6 %collective-permute-start.13 = (f32[1,64,1536]{2,1,0:T(8,128)S(1)}, f32[1,64,1536]{2,1,0:T(8,128)S(1)}, u32[]{:S(2)}, u32[]{:S(2)}) collective-permute-start(f32[1,64,1536]{2,1,0:T(8,128)S(1)} %broadcast_select_fusion.31), channel_id=31, source_target_pairs={{0,7},{1,0},{2,1},{3,2},{4,3},{5,4},{6,5},{7,6},{8,15},{9,8},{10,9... | collective-permute-start | bytes 1179656 | tf_op jit(solution)/vmap(transpose(jvp()))/dot_general | solution.py:21
  605.2 15.3 %collective-permute-start = (f32[1,64,1536]{2,1,0:T(8,128)S(1)}, f32[1,64,1536]{2,1,0:T(8,128)S(1)}, u32[]{:S(2)}, u32[]{:S(2)}) collective-permute-start(f32[1,64,1536]{2,1,0:T(8,128)S(1)} %broadcast_select_fusion.24), channel_id=14, source_target_pairs={{0,1},{1,2},{2,3},{3,4},{4,5},{5,6},{6,7},{7,0},{8,9},{9,10},{10,1... | collective-permute-start | bytes 1179656 | tf_op jit(solution)/vmap(transpose(jvp()))/dot_general | solution.py:20
  611.1 11.4 %collective-permute-start.1 = (f32[1,64,1536]{2,1,0:T(8,128)S(1)}, f32[1,64,1536]{2,1,0:T(8,128)S(1)}, u32[]{:S(2)}, u32[]{:S(2)}) collective-permute-start(f32[1,64,1536]{2,1,0:T(8,128)S(1)} %broadcast_select_fusion.25), channel_id=13, source_target_pairs={{0,7},{1,0},{2,1},{3,2},{4,3},{5,4},{6,5},{7,6},{8,15},{9,8},{10,9... | collective-permute-start | bytes 1179656 | tf_op jit(solution)/vmap(transpose(jvp()))/dot_general | solution.py:20
  622.6 12.6 %collective-permute-start.2 = (f32[1,64,1536]{2,1,0:T(8,128)S(1)}, f32[1,64,1536]{2,1,0:T(8,128)S(1)}, u32[]{:S(2)}, u32[]{:S(2)}) collective-permute-start(f32[1,64,1536]{2,1,0:T(8,128)S(1)} %get-tuple-element.461), channel_id=16, source_target_pairs={{0,1},{1,2},{2,3},{3,4},{4,5},{5,6},{6,7},{7,0},{8,9},{9,10},{10,1... | collective-permute-start | bytes 1179656 | tf_op jit(solution)/vmap(transpose(jvp()))/dot_general | solution.py:20
  625.1 10.9 %collective-permute-start.3 = (f32[1,64,1536]{2,1,0:T(8,128)S(1)}, f32[1,64,1536]{2,1,0:T(8,128)S(1)}, u32[]{:S(2)}, u32[]{:S(2)}) collective-permute-start(f32[1,64,1536]{2,1,0:T(8,128)S(1)} %get-tuple-element.462), channel_id=15, source_target_pairs={{0,7},{1,0},{2,1},{3,2},{4,3},{5,4},{6,5},{7,6},{8,15},{9,8},{10,9... | collective-permute-start | bytes 1179656 | tf_op jit(solution)/vmap(transpose(jvp()))/dot_general | solution.py:20
  637.8 12.7 %collective-permute-start = (f32[1,64,1536]{2,1,0:T(8,128)S(1)}, f32[1,64,1536]{2,1,0:T(8,128)S(1)}, u32[]{:S(2)}, u32[]{:S(2)}) collective-permute-start(f32[1,64,1536]{2,1,0:T(8,128)S(1)} %broadcast_select_fusion.24), channel_id=14, source_target_pairs={{0,1},{1,2},{2,3},{3,4},{4,5},{5,6},{6,7},{7,0},{8,9},{9,10},{10,1... | collective-permute-start | bytes 1179656 | tf_op jit(solution)/vmap(transpose(jvp()))/dot_general | solution.py:20
  639.6 10.9 %collective-permute-start.1 = (f32[1,64,1536]{2,1,0:T(8,128)S(1)}, f32[1,64,1536]{2,1,0:T(8,128)S(1)}, u32[]{:S(2)}, u32[]{:S(2)}) collective-permute-start(f32[1,64,1536]{2,1,0:T(8,128)S(1)} %broadcast_select_fusion.25), channel_id=13, source_target_pairs={{0,7},{1,0},{2,1},{3,2},{4,3},{5,4},{6,5},{7,6},{8,15},{9,8},{10,9... | collective-permute-start | bytes 1179656 | tf_op jit(solution)/vmap(transpose(jvp()))/dot_general | solution.py:20
  650.7 11.3 %collective-permute-start.2 = (f32[1,64,1536]{2,1,0:T(8,128)S(1)}, f32[1,64,1536]{2,1,0:T(8,128)S(1)}, u32[]{:S(2)}, u32[]{:S(2)}) collective-permute-start(f32[1,64,1536]{2,1,0:T(8,128)S(1)} %get-tuple-element.461), channel_id=16, source_target_pairs={{0,1},{1,2},{2,3},{3,4},{4,5},{5,6},{6,7},{7,0},{8,9},{9,10},{10,1... | collective-permute-start | bytes 1179656 | tf_op jit(solution)/vmap(transpose(jvp()))/dot_general | solution.py:20
  651.3 10.8 %collective-permute-start.3 = (f32[1,64,1536]{2,1,0:T(8,128)S(1)}, f32[1,64,1536]{2,1,0:T(8,128)S(1)}, u32[]{:S(2)}, u32[]{:S(2)}) collective-permute-start(f32[1,64,1536]{2,1,0:T(8,128)S(1)} %get-tuple-element.462), channel_id=15, source_target_pairs={{0,7},{1,0},{2,1},{3,2},{4,3},{5,4},{6,5},{7,6},{8,15},{9,8},{10,9... | collective-permute-start | bytes 1179656 | tf_op jit(solution)/vmap(transpose(jvp()))/dot_general | solution.py:20
  663.6 13.6 %collective-permute-start.4 = (f32[1,64,1536]{2,1,0:T(8,128)S(1)}, f32[1,64,1536]{2,1,0:T(8,128)S(1)}, u32[]{:S(2)}, u32[]{:S(2)}) collective-permute-start(f32[1,64,1536]{2,1,0:T(8,128)S(1)} %broadcast_select_fusion.26), channel_id=20, source_target_pairs={{0,1},{1,2},{2,3},{3,4},{4,5},{5,6},{6,7},{7,0},{8,9},{9,10},{10,1... | collective-permute-start | bytes 1179656 | tf_op jit(solution)/vmap(transpose(jvp()))/dot_general | solution.py:20
  664.5 12.8 %collective-permute-start.5 = (f32[1,64,1536]{2,1,0:T(8,128)S(1)}, f32[1,64,1536]{2,1,0:T(8,128)S(1)}, u32[]{:S(2)}, u32[]{:S(2)}) collective-permute-start(f32[1,64,1536]{2,1,0:T(8,128)S(1)} %broadcast_select_fusion.27), channel_id=19, source_target_pairs={{0,7},{1,0},{2,1},{3,2},{4,3},{5,4},{6,5},{7,6},{8,15},{9,8},{10,9... | collective-permute-start | bytes 1179656 | tf_op jit(solution)/vmap(transpose(jvp()))/dot_general | solution.py:20
  677.4 10.2 %collective-permute-start.6 = (f32[1,64,1536]{2,1,0:T(8,128)S(1)}, f32[1,64,1536]{2,1,0:T(8,128)S(1)}, u32[]{:S(2)}, u32[]{:S(2)}) collective-permute-start(f32[1,64,1536]{2,1,0:T(8,128)S(1)} %get-tuple-element.470), channel_id=22, source_target_pairs={{0,1},{1,2},{2,3},{3,4},{4,5},{5,6},{6,7},{7,0},{8,9},{9,10},{10,1... | collective-permute-start | bytes 1179656 | tf_op jit(solution)/vmap(transpose(jvp()))/dot_general | solution.py:20
  677.5 10.1 %collective-permute-start.7 = (f32[1,64,1536]{2,1,0:T(8,128)S(1)}, f32[1,64,1536]{2,1,0:T(8,128)S(1)}, u32[]{:S(2)}, u32[]{:S(2)}) collective-permute-start(f32[1,64,1536]{2,1,0:T(8,128)S(1)} %get-tuple-element.471), channel_id=21, source_target_pairs={{0,7},{1,0},{2,1},{3,2},{4,3},{5,4},{6,5},{7,6},{8,15},{9,8},{10,9... | collective-permute-start | bytes 1179656 | tf_op jit(solution)/vmap(transpose(jvp()))/dot_general | solution.py:20
  689.5 13.6 %collective-permute-start.4 = (f32[1,64,1536]{2,1,0:T(8,128)S(1)}, f32[1,64,1536]{2,1,0:T(8,128)S(1)}, u32[]{:S(2)}, u32[]{:S(2)}) collective-permute-start(f32[1,64,1536]{2,1,0:T(8,128)S(1)} %broadcast_select_fusion.26), channel_id=20, source_target_pairs={{0,1},{1,2},{2,3},{3,4},{4,5},{5,6},{6,7},{7,0},{8,9},{9,10},{10,1... | collective-permute-start | bytes 1179656 | tf_op jit(solution)/vmap(transpose(jvp()))/dot_general | solution.py:20
  690.8 12.3 %collective-permute-start.5 = (f32[1,64,1536]{2,1,0:T(8,128)S(1)}, f32[1,64,1536]{2,1,0:T(8,128)S(1)}, u32[]{:S(2)}, u32[]{:S(2)}) collective-permute-start(f32[1,64,1536]{2,1,0:T(8,128)S(1)} %broadcast_select_fusion.27), channel_id=19, source_target_pairs={{0,7},{1,0},{2,1},{3,2},{4,3},{5,4},{6,5},{7,6},{8,15},{9,8},{10,9... | collective-permute-start | bytes 1179656 | tf_op jit(solution)/vmap(transpose(jvp()))/dot_general | solution.py:20
  703.2 13.3 %collective-permute-start.6 = (f32[1,64,1536]{2,1,0:T(8,128)S(1)}, f32[1,64,1536]{2,1,0:T(8,128)S(1)}, u32[]{:S(2)}, u32[]{:S(2)}) collective-permute-start(f32[1,64,1536]{2,1,0:T(8,128)S(1)} %get-tuple-element.470), channel_id=22, source_target_pairs={{0,1},{1,2},{2,3},{3,4},{4,5},{5,6},{6,7},{7,0},{8,9},{9,10},{10,1... | collective-permute-start | bytes 1179656 | tf_op jit(solution)/vmap(transpose(jvp()))/dot_general | solution.py:20
  703.3 13.2 %collective-permute-start.7 = (f32[1,64,1536]{2,1,0:T(8,128)S(1)}, f32[1,64,1536]{2,1,0:T(8,128)S(1)}, u32[]{:S(2)}, u32[]{:S(2)}) collective-permute-start(f32[1,64,1536]{2,1,0:T(8,128)S(1)} %get-tuple-element.471), channel_id=21, source_target_pairs={{0,7},{1,0},{2,1},{3,2},{4,3},{5,4},{6,5},{7,6},{8,15},{9,8},{10,9... | collective-permute-start | bytes 1179656 | tf_op jit(solution)/vmap(transpose(jvp()))/dot_general | solution.py:20
  717.3 20.4 %collective-permute-start.27 = (f32[1,64,1536]{2,1,0:T(8,128)}, f32[1,64,1536]{2,1,0:T(8,128)S(1)}, u32[]{:S(2)}, u32[]{:S(2)}) collective-permute-start(f32[1,64,1536]{2,1,0:T(8,128)} %copy-done.23), channel_id=35, source_target_pairs={{0,1},{1,2},{2,3},{3,4},{4,5},{5,6},{6,7},{7,0},{8,9},{9,10},{10,1... | collective-permute-start | bytes 1179656 | tf_op jit(solution)/vmap(transpose(jvp()))/dot_general | solution.py:21
  733.6 11.7 %collective-permute-start.25 = (f32[1,64,1536]{2,1,0:T(8,128)S(1)}, f32[1,64,1536]{2,1,0:T(8,128)S(1)}, u32[]{:S(2)}, u32[]{:S(2)}) collective-permute-start(f32[1,64,1536]{2,1,0:T(8,128)S(1)} %copy-done.21), channel_id=23, source_target_pairs={{0,1},{1,2},{2,3},{3,4},{4,5},{5,6},{6,7},{7,0},{8,9},{9,10},{10,1... | collective-permute-start | bytes 1179656 | tf_op jit(solution)/vmap(transpose(jvp()))/dot_general | solution.py:20
  (52 other events, 739.5 us)
Sparse Core Ops, SparseCore 0:
  9.6 40.1 all-gather.28
  51.4 34.7 all-gather.30
  87.7 34.7 all-gather.32
  123.9 34.7 all-gather.36
  160.1 34.7 all-gather.38
  196.4 34.7 all-gather.34
where the time goes:
time: 760 us; the launch traced here: 753 us
  matrix products  325 us (43%)
  waiting for transfers between devices  145 us (19%)
  starting transfers between devices  88.2 us (12%)
  local copies, waits for them, and re-layouts  82.6 us (11%)
  other arithmetic  72.6 us (10%)
  loops' own time  25.5 us (3%)
  between operations  14.8 us (2%)
    dot_general x12, matrix products, layer(): gate = jnp.dot(a, w['w_gate'], preferred_element_type=jnp.float32)  126 us
    dot_general x12, matrix products, layer(): up = jnp.dot(a, w['w_up'], preferred_element_type=jnp.float32)  116 us
    squeeze x6, waiting for transfers between devices, stack(): h = layer(h, {name: w[number] for name, w in weights.items()})  95.4 us
    dot_general x11, matrix products, matmul(): jnp.dot(a, w, preferred_element_type=jnp.float32).astype(jnp.bfloat16)  82.8 us
    unnamed x71, local copies, waits for them, and re-layouts  67.8 us
    dot_general x18, starting transfers between devices, layer(): gate = jnp.dot(a, w['w_gate'], preferred_element_type=jnp.float32)  33 us
    convert_element_type x1, other arithmetic, layer(): (jax.nn.silu(gate) * up).astype(jnp.bfloat16)  32.6 us
    dot_general x18, waiting for transfers between devices, matmul(): jnp.dot(a, w, preferred_element_type=jnp.float32).astype(jnp.bfloat16)  29.8 us
  transfers between devices with their start and end apart: 60, of which 21 were waited for; matrix products, arithmetic and copies ran while one was open for 51% of the time, Pallas kernels for 0%

commit v1 on v0

v1 whole, which is shorter than its diff:
```python
import functools

import jax
import jax.numpy as jnp
from jax import lax
from jax.experimental import pallas as pl
from jax.experimental.pallas import tpu as pltpu
from jax.sharding import PartitionSpec as P

BF = jnp.bfloat16
F32 = jnp.float32
CHUNKS = 3
TM = 256
EPS = 1e-6
VMEM_LIMIT = 67043328


def dot(a, b):
    return lax.dot_general(a, b, (((1,), (0,)), ((), ())), preferred_element_type=F32)


def dot_nt(a, b):
    return lax.dot_general(a, b, (((1,), (1,)), ((), ())), preferred_element_type=F32)


def dot_tn(a, b):
    return lax.dot_general(a, b, (((0,), (0,)), ((), ())), preferred_element_type=F32)


def sigmoid(g):
    return 0.5 * jnp.tanh(0.5 * g) + 0.5


def scale_of(wide):
    return lax.rsqrt(jnp.mean(wide * wide, -1, keepdims=True) + EPS)


def normed(wide):
    return (wide * scale_of(wide)).astype(BF)


def aligned(start, size):
    return pl.ds(pl.multiple_of(start, size), size)


def kernel(x_hbm, dy_hbm, w_hbm, dx_hbm, terms_hbm, h_hbm, a, y, g, w, acc, act0, act1, g0, g1, terms, io, sem, io_sem):
    layers, chunks = w.shape[:2]
    tokens, d = y.shape
    fc = w.shape[-1]
    half = fc // 2
    nt = tokens // TM
    big = io.shape[1]
    acts, gs = (act0, act1), (g0, g1)

    loads = [pltpu.make_async_copy(x_hbm, a.at[0], sem.at[0]), pltpu.make_async_copy(dy_hbm, y, sem.at[1]), pltpu.make_async_copy(w_hbm, w, sem.at[2])]
    for copy in loads:
        copy.start()
    loads[0].wait()

    def norm_x(t, _):
        rows = aligned(t * TM, TM)
        a[0, rows, :] = normed(a[0, rows, :].astype(F32))
        return 0

    lax.fori_loop(0, nt, norm_x, 0)
    loads[2].wait()

    def hidden(j, _):
        c, t = j // (nt // 4), j % (nt // 4)
        for k in range(4):
            rows = aligned((4 * t + k) * TM, TM)
            at = a[0, rows, :]
            for f in (0, half):
                gate = dot(at, w[0, c, 0, :, f : f + half])
                up = dot(at, w[0, c, 1, :, f : f + half])
                g[c, rows, f : f + half] = (gate * sigmoid(gate) * up).astype(BF)
        return 0

    lax.fori_loop(0, chunks * nt // 4, hidden, 0)

    steps = tokens // big

    def io_in(src, j):
        return pltpu.make_async_copy(src.at[aligned(j * big, big), :], io.at[j % 2], io_sem.at[0, j % 2])

    def io_out(j):
        return pltpu.make_async_copy(io.at[j % 2], h_hbm.at[aligned(j * big, big), :], io_sem.at[1, j % 2])

    io_in(x_hbm, 0).start()

    def down(j, _):
        io_in(x_hbm, j).wait()

        @pl.when(j >= 1)
        def _():
            io_out(j - 1).wait()

        @pl.when(j + 1 < steps)
        def _():
            io_in(x_hbm, j + 1).start()

        for k in range(big // TM):
            rows = aligned(j * big + k * TM, TM)
            out = sum(dot(g[c, rows, :fc], w[0, c, 2]) for c in range(chunks))
            here = pl.ds(k * TM, TM)
            h = (io[j % 2, here, :].astype(F32) + out.astype(BF).astype(F32)).astype(BF)
            io[j % 2, here, :] = h
            a[1, rows, :] = normed(h.astype(F32))
        io_out(j).start()
        return 0

    lax.fori_loop(0, steps, down, 0)
    io_out(steps - 1).wait()
    loads[1].wait()

    for l in range(layers):
        for m in range(3):
            acc[m] = jnp.zeros_like(acc[m])

    def backward(turn, _):
        l = layers - 1 - turn

        def grads_in(i, slot, f):
            c, t = i // nt, i % nt
            rows = aligned(t * TM, TM)
            at, dt = a[l, rows, :], y[rows, :]
            gate = dot(at, w[l, c, 0, :, f : f + half])
            up = dot(at, w[l, c, 1, :, f : f + half])
            dact = dot_nt(dt, w[l, c, 2, f : f + half, :]).astype(BF).astype(F32)
            s = sigmoid(gate)
            silu = gate * s
            acts[slot][:, f : f + half] = (silu * up).astype(BF)
            dgate = (dact * up * (s + silu * (1.0 - s))).astype(BF)
            dup = (dact * silu).astype(BF)
            gs[slot][:, f : f + half] = dgate
            gs[slot][:, fc + f : fc + f + half] = dup
            g[c, rows, f : f + half] = dgate
            g[c, rows, fc + f : fc + f + half] = dup

        def down_grad(i, slot):
            rows = aligned(i % nt * TM, TM)
            acc[2] += dot_tn(acts[slot][...], y[rows, :])

        def in_grads(i, slot):
            rows = aligned(i % nt * TM, TM)
            at = a[l, rows, :]
            acc[0] += dot_tn(at, gs[slot][:, :fc])
            acc[1] += dot_tn(at, gs[slot][:, fc:])

        for f in (0, half):
            grads_in(0, 0, f)

        def chunk(c, _):
            def body(j, _):
                for k in range(4):
                    i = 4 * j + k
                    later = jnp.minimum(i + 1, chunks * nt - 1)
                    grads_in(later, (k + 1) % 2, 0)
                    down_grad(i, k % 2)
                    grads_in(later, (k + 1) % 2, half)
                    in_grads(i, k % 2)
                return 0

            lax.fori_loop(c * nt // 4, (c + 1) * nt // 4, body, 0)
            for m in range(3):
                terms[c, m] = acc[m].astype(BF)
                acc[m] = jnp.zeros_like(acc[m])
            return 0

        lax.fori_loop(0, chunks, chunk, 0)

        out = pltpu.make_async_copy(terms, terms_hbm.at[l], sem.at[3])
        out.start()

        def fetch(j):
            @pl.when(l == 0)
            def _():
                io_in(x_hbm, j).start()

            @pl.when(l != 0)
            def _():
                io_in(h_hbm, j).start()

        def dx_out(j):
            rows = aligned(j * big, big)
            return pltpu.make_async_copy(y.at[rows, :], dx_hbm.at[rows, :], io_sem.at[1, j % 2])

        fetch(0)

        def inputs(j, _):
            io_in(x_hbm, j).wait()

            @pl.when(j + 1 < steps)
            def _():
                fetch(j + 1)

            for k in range(big // TM):
                rows = aligned(j * big + k * TM, TM)
                da = sum(dot_nt(g[c, rows, m * fc : (m + 1) * fc], w[l, c, m]) for c in range(chunks) for m in range(2))
                da = da.astype(BF).astype(F32)
                wide = io[j % 2, pl.ds(k * TM, TM), :].astype(F32)
                scale = scale_of(wide)
                along = jnp.mean(da * wide, -1, keepdims=True) * (scale * scale * scale)
                dh = (da * scale - wide * along).astype(BF).astype(F32)
                y[rows, :] = (y[rows, :].astype(F32) + dh).astype(BF)

            @pl.when(l == 0)
            def _():
                dx_out(j).start()

            return 0

        lax.fori_loop(0, steps, inputs, 0)
        out.wait()

        @pl.when(l == 0)
        def _():
            for j in range(steps):
                dx_out(j).wait()

        return 0

    lax.fori_loop(0, layers, backward, 0)


def layers_of(x, dy, w):
    tokens, d = x.shape
    layers, chunks, _, _, fc = w.shape
    big = 4 * TM
    hbm = pl.BlockSpec(memory_space=pl.ANY)
    return pl.pallas_call(
        kernel,
        out_shape=(
            jax.ShapeDtypeStruct(x.shape, BF),
            jax.ShapeDtypeStruct(w.shape, BF),
            jax.ShapeDtypeStruct(x.shape, BF),
        ),
        in_specs=[hbm] * 3,
        out_specs=[hbm] * 3,
        scratch_shapes=[
            pltpu.VMEM((layers, tokens, d), BF),
            pltpu.VMEM((tokens, d), BF),
            pltpu.VMEM((chunks, tokens, 2 * fc), BF),
            pltpu.VMEM(w.shape, BF),
            pltpu.VMEM((3, d, fc), F32),
            pltpu.VMEM((TM, fc), BF),
            pltpu.VMEM((TM, fc), BF),
            pltpu.VMEM((TM, 2 * fc), BF),
            pltpu.VMEM((TM, 2 * fc), BF),
            pltpu.VMEM(w.shape[1:], BF),
            pltpu.VMEM((2, big, d), BF),
            pltpu.SemaphoreType.DMA((4,)),
            pltpu.SemaphoreType.DMA((2, 2)),
        ],
        compiler_params=pltpu.CompilerParams(vmem_limit_bytes=VMEM_LIMIT, has_side_effects=True),
        name="layers",
    )(x, dy, w)


def solution(mesh):
    n = mesh.shape["dp"]

    def local(x, dy, gate, up, down):
        layers, rows, ff = gate.shape
        d = x.shape[-1]
        own = ff // n // CHUNKS

        def columns(t):
            t = lax.all_gather(t, "dp", axis=1, tiled=True)
            t = t.reshape(layers, d, n, CHUNKS, own)
            return t.transpose(0, 3, 1, 2, 4).reshape(layers, CHUNKS, d, n * own)

        def rows_of(t):
            t = lax.all_gather(t, "dp", axis=1, tiled=True)
            t = t.reshape(layers, n, CHUNKS, own, d)
            return t.transpose(0, 2, 1, 3, 4).reshape(layers, CHUNKS, n * own, d)

        w = jnp.stack([columns(gate), columns(up), rows_of(down)], 2)
        dx, terms, _ = layers_of(x[0], dy[0], w)

        def back_columns(t):
            t = t.reshape(layers, CHUNKS, d, n, own).transpose(0, 2, 3, 1, 4).reshape(layers, d, ff)
            return lax.psum_scatter(t, "dp", scatter_dimension=1, tiled=True)

        def back_rows(t):
            t = t.reshape(layers, CHUNKS, n, own, d).transpose(0, 2, 1, 3, 4).reshape(layers, ff, d)
            return lax.psum_scatter(t, "dp", scatter_dimension=1, tiled=True)

        return dx[None], back_columns(terms[:, :, 0]), back_columns(terms[:, :, 1]), back_rows(terms[:, :, 2])

    both, rows = P(("rep", "dp"), None, None), P(None, "dp", None)
    return jax.shard_map(
        local, mesh=mesh, in_specs=(both, both, rows, rows, rows),
        out_specs=(both, P("rep", "dp", None), P("rep", "dp", None), P("rep", "dp", None)), check_vma=False,
    )
```

time: 760 us -> 541 us (0.71)
  matrix products: 325 us -> 0 us
  Pallas kernels: 0 us -> 159 us
  waiting for transfers between devices: 145 us -> 278 us
  starting transfers between devices: 88.2 us -> 0.32 us
  other arithmetic: 72.6 us -> 4.44 us
  loops' own time: 25.5 us -> 0 us
    dot_general x35 -> x0, matrix products: 325 us -> none  [the longest x12 126 us: layer(): gate = jnp.dot(a, w['w_gate'], preferred_element_type=jnp.float32)]
    pallas_call x0 -> x1, Pallas kernels: none -> 159 us  [layers_of(): pl.pallas_call(kernel, out_shape=(jax.ShapeDtypeStruct(x.shape, BF), jax....]
    unnamed x6, waiting for transfers between devices: 1.85 us -> 138 us
    all_gather x0 -> x3, waiting for transfers between devices: none -> 98.6 us  [the longest x2 73.7 us: columns(): t = lax.all_gather(t, 'dp', axis=1, tiled=True)]
    squeeze x6 -> x0, waiting for transfers between devices: 95.4 us -> none  [stack(): h = layer(h, {name: w[number] for name, w in weights.items()})]
    dot_general x54 -> x0, starting transfers between devices: 87.8 us -> none  [the longest x18 33 us: layer(): gate = jnp.dot(a, w['w_gate'], preferred_element_type=jnp.float32)]
    unnamed x71 -> x10, local copies, waits for them, and re-layouts: 67.8 us -> 9.14 us
    dot_general x54 -> x0, waiting for transfers between devices: 47.5 us -> none  [the longest x18 29.8 us: matmul(): jnp.dot(a, w, preferred_element_type=jnp.float32).astype(jnp.bfloat16)]
  transfers between devices with their start and end apart: 60 -> 5, of which waited for: 21 -> 5; matrix products, arithmetic and copies ran while one was open for 51% -> 7% of each run, Pallas kernels for 0% -> 0%
where the time goes in v1:
time: 541 us; the launch traced here: 540 us
  waiting for transfers between devices  278 us (51%)
  Pallas kernels  159 us (29%)
  local copies, waits for them, and re-layouts  83.4 us (15%)
  between operations  14.5 us (3%)
    pallas_call x1, Pallas kernels, layers_of(): pl.pallas_call(kernel, out_shape=(jax.ShapeDtypeStruct(x.shape, BF), jax....  159 us
    unnamed x6, waiting for transfers between devices  138 us
    all_gather x2, waiting for transfers between devices, columns(): t = lax.all_gather(t, 'dp', axis=1, tiled=True)  73.7 us
    reduce_scatter x1, waiting for transfers between devices, back_rows(): return lax.psum_scatter(t, 'dp', scatter_dimension=1, tiled=True)  41.5 us
    all_gather x1, waiting for transfers between devices, rows_of(): t = lax.all_gather(t, 'dp', axis=1, tiled=True)  24.9 us
    reshape x2, local copies, waits for them, and re-layouts, back_columns(): t.reshape(layers, CHUNKS, d, n, own).transpose(0, 2, 3, 1, 4)  17.6 us
    all_gather x2, local copies, waits for them, and re-layouts, columns(): t = lax.all_gather(t, 'dp', axis=1, tiled=True)  15.6 us
  transfers between devices with their start and end apart: 5, of which 5 were waited for; matrix products, arithmetic and copies ran while one was open for 7% of the time, Pallas kernels for 0%

profile of v1, /device:TPU:22, one launch (start us, length us, event | category | flops | bytes accessed | tf_op | source)
XLA Modules:
  0.0 539.9 jit_solution(17880561979459776180)
XLA Ops:
  7.2 0.1 all-gather.4.cloned.1.call-start
  7.2 2.1 copy.29
  9.4 0.1 all-gather.4.cloned.1.call-update
  9.5 0.1 all-gather.6.cloned.1.call-start
  9.5 2.1 copy.32
  11.7 0.1 all-gather.6.cloned.1.call-update
  11.7 0.1 all-gather.8.cloned.1.call-start
  11.8 0.7 all-gather.8.cloned.1.call-update
  12.5 0.1 all-reduce.5.cloned.1.call-start
  12.6 43.2 %all-gather.4.cloned.1.call-done = bf16[2,512,1536]{2,0,1:T(2,128)(2,1)} async-done(((bf16[2,64,1536]{2,0,1:T(2,128)(2,1)}), bf16[2,512,1536]{2,0,1:T(2,128)(2,1)}) %all-gather.4.cloned.1.call-update) | async-done | bytes 3145744 | tf_op jit(solution)/shard_map/all_gather | solution.py:269
  55.8 7.0 %copy.30 = bf16[2,512,1536]{1,2,0:T(8,128)(2,1)S(1)} copy(bf16[2,512,1536]{2,0,1:T(2,128)(2,1)} %all-gather.4.cloned.1.call-done) | data formatting | bytes 6291456 | tf_op jit(solution)/shard_map/all_gather | solution.py:269
  62.8 1.9 copy.31
  64.7 3.2 copy.36
  67.9 30.5 %all-gather.6.cloned.1.call-done = bf16[2,512,1536]{2,0,1:T(2,128)(2,1)} async-done(((bf16[2,64,1536]{2,0,1:T(2,128)(2,1)}), bf16[2,512,1536]{2,0,1:T(2,128)(2,1)}) %all-gather.6.cloned.1.call-update) | async-done | bytes 3145744 | tf_op jit(solution)/shard_map/all_gather | solution.py:269
  98.4 8.6 %copy.33 = bf16[2,512,1536]{1,2,0:T(8,128)(2,1)} copy(bf16[2,512,1536]{2,0,1:T(2,128)(2,1)} %all-gather.6.cloned.1.call-done) | data formatting | bytes 6291456 | tf_op jit(solution)/shard_map/all_gather | solution.py:269
  107.0 3.9 copy.34
  111.0 4.6 copy.37
  115.6 24.9 %all-gather.8.cloned.1.call-done = bf16[2,1536,512]{2,1,0:T(8,128)(2,1)} async-done(((bf16[2,192,512]{2,1,0:T(8,128)(2,1)}), bf16[2,1536,512]{2,1,0:T(8,128)(2,1)}) %all-gather.8.cloned.1.call-update) | async-done | bytes 3145744 | tf_op jit(solution)/shard_map/all_gather | solution.py:274
  140.5 0.0 copy-start
  140.5 2.4 copy.35
  142.9 0.4 copy-done
  143.3 4.4 pad_maximum_fusion.w_hbm
  147.8 159.4 %layers.1 = (bf16[4096,512]{1,0:T(8,128)(2,1)}, bf16[2,3,3,512,512]{4,3,2,1,0:T(8,128)(2,1)}, bf16[4096,512]{1,0:T(8,128)(2,1)}) custom-call(bf16[4096,512]{1,0:T(8,128)(2,1)} %bitcast.39, bf16[4096,512]{1,0:T(8,128)(2,1)} %bitcast.40, bf16[2,3,3,512,512]{4,3,2,1,0:T(8,128)(2,1)} %pad_maximum_fusion.w_hbm), custom_call_target="tpu_custom_call" | custom-call | tf_op jit(solution)/shard_map/layers/pallas_call | solution.py:231
  307.2 5.9 %fusion = (bf16[2,3,1,512,512]{4,3,2,1,0:T(8,128)(2,1)S(1)}, bf16[2,3,1,512,512]{4,3,2,1,0:T(8,128)(2,1)}, bf16[2,3,1,512,512]{4,3,2,1,0:T(8,128)(2,1)}) fusion(bf16[2,3,3,512,512]{4,3,2,1,0:T(8,128)(2,1)} %get-tuple-element.7), kind=kLoop, calls=%fused_computation.3 | loop fusion | bytes 18874368 | tf_op jit(solution)/shard_map/slice | solution.py:289
  313.1 4.7 copy.38
  317.8 3.9 copy.39
  321.8 8.8 %copy.40 = bf16[2,512,1536]{2,0,1:T(2,128)(2,1)} copy(bf16[2,512,1536]{1,2,0:T(8,128)(2,1)} %bitcast.36) | data formatting | bytes 6291456 | tf_op jit(solution)/shard_map/reshape | solution.py:282
  330.5 4.7 copy.41
  335.2 3.9 copy.42
  339.2 8.8 %copy.43 = bf16[2,512,1536]{2,0,1:T(2,128)(2,1)} copy(bf16[2,512,1536]{1,2,0:T(8,128)(2,1)} %bitcast.38) | data formatting | bytes 6291456 | tf_op jit(solution)/shard_map/reshape | solution.py:282
  348.0 0.1 all-reduce.5.cloned.1.call-update
  348.1 0.1 reduce-scatter.2.cloned.1.call-start
  348.1 1.9 copy.44
  350.0 0.0 copy-start.1
  350.0 0.1 reduce-scatter.2.cloned.1.call-update
  350.1 0.6 copy-done.1
  350.7 0.6 dynamic-slice
  351.9 136.7 %all-reduce.5.cloned.1.call-done = (bf16[2,512,1536]{2,0,1:T(2,128)(2,1)}, bf16[2,512,1536]{2,0,1:T(2,128)(2,1)}) async-done(((bf16[2,512,1536]{2,0,1:T(2,128)(2,1)}, bf16[2,512,1536]{2,0,1:T(2,128)(2,1)}), (bf16[2,512,1536]{2,0,1:T(2,128)(2,1)}, bf16[2,512,1536]{2,0,1:T(2,128)(2,1)})) %all-reduce.5.cloned.1.call-update) | async-done | bytes 6291472
  488.6 1.7 constant_dynamic-slice_fusion
  490.3 0.8 copy.45
  491.1 0.8 copy.46
  491.8 41.5 %reduce-scatter.2.cloned.1.call-done = bf16[2,192,512]{2,1,0:T(8,128)(2,1)} async-done(((bf16[2,1536,512]{2,1,0:T(8,128)(2,1)}), bf16[2,192,512]{2,1,0:T(8,128)(2,1)}) %reduce-scatter.2.cloned.1.call-update) | async-done | bytes 393232 | tf_op jit(solution)/shard_map/reduce_scatter | solution.py:287
Async XLA Ops:
  7.2 48.6 %all-gather.4.cloned.1.call-start = ((), (), s32[]{:S(2)}) async-start(), calls=%async_computation.1 | async-start | bytes 3538944 | tf_op jit(solution)/shard_map/all_gather | solution.py:269
  9.5 89.0 %all-gather.6.cloned.1.call-start = ((), (), s32[]{:S(2)}) async-start(), calls=%async_computation.2 | async-start | bytes 3538944 | tf_op jit(solution)/shard_map/all_gather | solution.py:269
  11.7 128.8 %all-gather.8.cloned.1.call-start = ((), (), s32[]{:S(2)}) async-start(), calls=%async_computation.3 | async-start | bytes 3538944 | tf_op jit(solution)/shard_map/all_gather | solution.py:274
  12.5 476.1 %all-reduce.5.cloned.1.call-start = ((), (), s32[]{:S(2)}) async-start(), calls=%async_computation.5 | async-start | bytes 12582912
  140.5 2.8 copy-start
  348.1 185.3 %reduce-scatter.2.cloned.1.call-start = ((), (), s32[]{:S(2)}) async-start(), calls=%async_computation.4 | async-start | bytes 3538944 | tf_op jit(solution)/shard_map/reduce_scatter | solution.py:287
  350.0 0.7 copy-start.1
Sparse Core Ops, SparseCore 0:
  10.2 45.5 all-gather.3
  57.9 40.4 all-gather.5
  100.0 40.4 all-gather.7
  348.2 140.3 all-reduce.4
  491.4 41.9 reduce-scatter.1

commit v2 on v1

v2 whole, which is shorter than its diff:
```python
import functools

import jax
import jax.numpy as jnp
from jax import lax
from jax.experimental import pallas as pl
from jax.experimental.pallas import tpu as pltpu
from jax.sharding import PartitionSpec as P

BF = jnp.bfloat16
F32 = jnp.float32
CHUNKS = 3
TILES = 16
EPS = 1e-6
VMEM_LIMIT = 67043328


def dot(a, b):
    return lax.dot_general(a, b, (((1,), (0,)), ((), ())), preferred_element_type=F32)


def dot_nt(a, b):
    return lax.dot_general(a, b, (((1,), (1,)), ((), ())), preferred_element_type=F32)


def dot_tn(a, b):
    return lax.dot_general(a, b, (((0,), (0,)), ((), ())), preferred_element_type=F32)


def sigmoid(g):
    return 0.5 * jnp.tanh(0.5 * g) + 0.5


def scale_of(wide):
    return lax.rsqrt(jnp.mean(wide * wide, -1, keepdims=True) + EPS)


def normed(wide):
    return (wide * scale_of(wide)).astype(BF)


def aligned(start, size):
    return pl.ds(pl.multiple_of(start, size), size)


def kernel(
    n, x_hbm, dy_hbm, gate_hbm, up_hbm, down_hbm, dx_hbm, dgate_hbm, dup_hbm, ddown_hbm, h_hbm,
    a, y, g, w, acc, act0, act1, g0, g1, terms, slots, fin, fixed, io,
    sem, io_sem, out_sem, ag_recv, ag_send, side_recv, rs_recv, rs_send, credit,
):
    layers, chunks = w.shape[:2]
    tokens, d = y.shape
    fc = w.shape[-1]
    own = d // n
    half = fc // 2
    tm = tokens // TILES
    big = 2 * tm
    per = TILES // 2
    acts, gs = (act0, act1), (g0, g1)
    near = (n - 1) // 2
    items = layers * chunks * 3

    me = lax.axis_index("dp")
    core = lax.axis_index("rep") % 2
    left, right = {"dp": (me + n - 1) % n}, {"dp": (me + 1) % n}
    partner = {"rep": lax.axis_index("rep") + 1 - 2 * core}

    def place(c, m, s):
        return s + jnp.where((m == 2) & (c == 1), 1 - 2 * (s % 2), 0)

    def remote(src, dst, send, recv, to):
        return pltpu.make_async_remote_copy(src, dst, send, recv, device_id=to, device_id_type=pl.DeviceIdType.MESH)

    def item(i):
        l, r = i // (chunks * 3), i % (chunks * 3)
        first = l == 0
        c = jnp.where(first, jnp.where(r < 2 * chunks, r // 2, r - 2 * chunks), r // 3)
        m = jnp.where(first, jnp.where(r < 2 * chunks, r % 2, 2), r % 3)
        return l, c, m

    def gather(k):
        def hop(back, _):
            h = near + 1 - back
            i = k - 2 * h

            @pl.when((i >= 0) & (i < items))
            def _():
                l, c, m = item(i)
                far = near + i % 2

                def way(side, _):
                    reach = jnp.where(side == 0, far, n - 1 - far)
                    s = jnp.where(side == 0, me + n - h, me + h) % n
                    rows = aligned(place(c, m, s) * own + core * (own // 2), own // 2)
                    ref = w.at[l, c, m, rows, :]
                    at = jnp.where(side == 0, 0, far) + h
                    to = {"dp": jnp.where(side == 0, me + 1, me + n - 1) % n}

                    @pl.when((h >= 1) & (h <= reach))
                    def _():
                        remote(ref, ref, ag_send.at[i], ag_recv.at[i, at - 1], to).wait_recv()

                    @pl.when(h < reach)
                    def _():
                        remote(ref, ref, ag_send.at[i], ag_recv.at[i, at], to).start()

                    @pl.when((h >= 1) & (h <= reach))
                    def _():
                        remote(ref, ref, ag_send.at[i], side_recv.at[i], partner).start()

                    return 0

                lax.fori_loop(0, 2, way, 0)

            return 0

        lax.fori_loop(0, near + 2, hop, 0)

    def arrived(i):
        l, c, m = item(i)
        ref = w.at[l, c, m, pl.ds(0, (n - 1) * (own // 2)), :]
        pltpu.make_async_copy(ref, ref, side_recv.at[i]).wait()

    def reduce(turn, q):
        late = q >= per

        def unit(u, _):
            base = jnp.where(late, q - per - u, q + 3 * per - u)
            t = jnp.where(late, turn, turn - 1)
            p = (2 * (base + 3)) % 3
            since = base - per * p
            s = since // 3

            @pl.when((t >= 0) & (since >= 0) & (since <= 3 * (near + 1)))
            def _():
                far = near + (p + u) % 2

                def way(side, _):
                    reach = jnp.where(side == 0, far, n - 1 - far)
                    at = jnp.where(side == 0, 0, far) + s
                    to = {"dp": jnp.where(side == 0, me + 1, me + n - 1) % n}
                    o = jnp.where(side == 0, me + reach - s, me + n - reach + s) % n
                    rows = aligned(place(p, u, o) * own, own)

                    @pl.when((s == 0) & (t >= 1))
                    def _():
                        pl.semaphore_wait(credit.at[side, p, u], 1)

                    @pl.when(s == 0)
                    def _():
                        remote(terms.at[p, u, rows, :], slots.at[p, u, at], rs_send.at[p, u], rs_recv.at[p, u, at], to).start()

                    @pl.when((s >= 1) & (s < reach))
                    def _():
                        ref = slots.at[p, u, at - 1]
                        remote(ref, ref, rs_send.at[p, u], rs_recv.at[p, u, at - 1], to).wait_recv()
                        ref[...] = (ref[...].astype(F32) + terms[p, u, rows, :].astype(F32)).astype(BF)
                        remote(ref, slots.at[p, u, at], rs_send.at[p, u], rs_recv.at[p, u, at], to).start()

                    return 0

                lax.fori_loop(0, 2, way, 0)

                @pl.when(s == near + 1)
                def _():
                    finish(t, p, u, far)

            return 0

        lax.fori_loop(0, 3, unit, 0)

    def down_out(l, p):
        return pltpu.make_async_copy(fin.at[p, 2], ddown_hbm.at[l, aligned(p * own, own), :], out_sem.at[p])

    def in_out(l, m, j):
        out = dgate_hbm if m == 0 else dup_hbm
        return pltpu.make_async_copy(fixed.at[m, j], out.at[l, :, pl.ds(j * d, d)], out_sem.at[chunks + m * chunks + j])

    def finish(t, p, u, far):
        l = layers - 1 - t
        ends = [slots.at[p, u, far - 1], slots.at[p, u, n - 2]]
        for ref, at in zip(ends, (far - 1, n - 2)):
            remote(ref, ref, rs_send.at[p, u], rs_recv.at[p, u, at], right).wait_recv()

        @pl.when((t >= 1) & (u == 2))
        def _():
            down_out(l, p).wait()

        rows = aligned(place(p, u, me) * own, own)
        fin[p, u] = (ends[0][...].astype(F32) + ends[1][...].astype(F32) + terms[p, u, rows, :].astype(F32)).astype(BF)
        ref = w.at[0, 0, 0, pl.ds(0, (n - 1) * own), :]
        pltpu.make_async_copy(ref, ref, rs_send.at[p, u]).wait()

        @pl.when(t < layers - 1)
        def _():
            pl.semaphore_signal(credit.at[0, p, u], 1, device_id=left, device_id_type=pl.DeviceIdType.MESH)
            pl.semaphore_signal(credit.at[1, p, u], 1, device_id=right, device_id_type=pl.DeviceIdType.MESH)

        @pl.when(u == 2)
        def _():
            down_out(l, p).start()

        @pl.when((u == 2) & (p == chunks - 1))
        def _():
            outs = [in_out(l, m, j) for m in range(2) for j in range(3)]

            @pl.when(t >= 1)
            def _():
                for copy in outs:
                    copy.wait()

            low = lax.broadcasted_iota(jnp.int32, (own, 128), 1) < 64
            for m in range(2):
                for e in range(fc // 128):
                    c0, c1, c2 = (fin[c, m, :, pl.ds(128 * e, 128)].astype(F32) for c in range(chunks))
                    for k, (lo, hi) in enumerate(((c0, c1), (c2, c0), (c1, c2))):
                        j, at = divmod(3 * e + k, d // 128)
                        fixed[m, j, :, pl.ds(128 * at, 128)] = jnp.where(low, lo, hi).astype(BF)
            for copy in outs:
                copy.start()

    shards = (gate_hbm, up_hbm)
    raw = [
        pltpu.make_async_copy(shards[m].at[l, :, pl.ds(j * d, d)], terms.at[l, m, pl.ds(j * own, own), :], sem.at[2 + (l * 2 + m) * 3 + j])
        for l in range(layers) for m in range(2) for j in range(3)
    ]
    downs = [
        pltpu.make_async_copy(down_hbm.at[l, pl.ds(c * own, own), :], w.at[l, c, 2, aligned(place(c, 2, me) * own, own), :], sem.at[2 + layers * 6 + l * 3 + c])
        for l in range(layers) for c in range(chunks)
    ]
    load_x, load_dy = pltpu.make_async_copy(x_hbm, a.at[0], sem.at[0]), pltpu.make_async_copy(dy_hbm, y, sem.at[1])
    for copy in (*raw, *downs, load_x, load_dy):
        copy.start()
    barrier = pltpu.get_barrier_semaphore()
    for to in (left, right, partner):
        pl.semaphore_signal(barrier, 1, device_id=to, device_id_type=pl.DeviceIdType.MESH)
    for copy in (*raw, *downs):
        copy.wait()
    low = lax.broadcasted_iota(jnp.int32, (own, 128), 1) < 64
    mine = aligned(me * own, own)
    for l in range(layers):
        for m in range(2):
            for e in range(fc // 128):
                parts = []
                for k in range(3):
                    j, at = divmod(3 * e + k, d // 128)
                    parts.append(terms[l, m, pl.ds(j * own, own), pl.ds(128 * at, 128)].astype(F32))
                k0, k1, k2 = parts
                for c, (lo, hi) in enumerate(((k0, k1), (k2, k0), (k1, k2))):
                    w[l, c, m, mine, pl.ds(128 * e, 128)] = jnp.where(low, lo, hi).astype(BF)
    pl.semaphore_wait(barrier, 3)

    def gather_some(k, _):
        gather(k)
        return 0

    lax.fori_loop(0, 2, gather_some, 0)
    load_x.wait()

    def norm_x(t, _):
        rows = aligned(t * tm, tm)
        a[0, rows, :] = normed(a[0, rows, :].astype(F32))
        return 0

    lax.fori_loop(0, TILES, norm_x, 0)
    done = 2 * (near + 1)
    lax.fori_loop(2, done + 2, gather_some, 0)

    bodies = TILES // 4

    def hidden(j, _):
        c, t = j // bodies, j % bodies

        @pl.when(j % 2 == 1)
        def _():
            gather(done + 2 + j // 2)

        @pl.when(t == 0)
        def _():
            arrived(2 * c)
            arrived(2 * c + 1)

        for k in range(4):
            rows = aligned((4 * t + k) * tm, tm)
            at = a[0, rows, :]
            for f in (0, half):
                gate = dot(at, w[0, c, 0, :, f : f + half])
                up = dot(at, w[0, c, 1, :, f : f + half])
                g[c, rows, f : f + half] = (gate * sigmoid(gate) * up).astype(BF)
        return 0

    lax.fori_loop(0, chunks * bodies, hidden, 0)

    def io_in(src, j):
        return pltpu.make_async_copy(src.at[aligned(j * big, big), :], io.at[j % 2], io_sem.at[0, j % 2])

    def io_out(j):
        return pltpu.make_async_copy(io.at[j % 2], h_hbm.at[aligned(j * big, big), :], io_sem.at[1, j % 2])

    later = done + 2 + chunks * bodies // 2
    io_in(x_hbm, 0).start()
    gather(later)
    for c in range(chunks):
        arrived(2 * chunks + c)

    def down(j, _):
        @pl.when((j % 2 == 0) & (j >= 2))
        def _():
            gather(later + j // 2)

        io_in(x_hbm, j).wait()

        @pl.when(j >= 1)
        def _():
            io_out(j - 1).wait()

        @pl.when(j + 1 < per)
        def _():
            io_in(x_hbm, j + 1).start()

        for k in range(2):
            rows = aligned(j * big + k * tm, tm)
            out = sum(dot(g[c, rows, :fc], w[0, c, 2]) for c in range(chunks))
            here = pl.ds(k * tm, tm)
            h = (io[j % 2, here, :].astype(F32) + out.astype(BF).astype(F32)).astype(BF)
            io[j % 2, here, :] = h
            a[1, rows, :] = normed(h.astype(F32))
        io_out(j).start()
        return 0

    lax.fori_loop(0, per, down, 0)
    last = later + per // 2
    io_out(per - 1).wait()
    load_dy.wait()

    for m in range(3):
        acc[m] = jnp.zeros_like(acc[m])

    def backward(turn, _):
        l = layers - 1 - turn

        def grads_in(i, slot, f):
            c, t = i // TILES, i % TILES
            rows = aligned(t * tm, tm)
            at, dt = a[l, rows, :], y[rows, :]
            gate = dot(at, w[l, c, 0, :, f : f + half])
            up = dot(at, w[l, c, 1, :, f : f + half])
            dact = dot_nt(dt, w[l, c, 2, f : f + half, :]).astype(BF).astype(F32)
            s = sigmoid(gate)
            silu = gate * s
            acts[slot][:, f : f + half] = (silu * up).astype(BF)
            dgate = (dact * up * (s + silu * (1.0 - s))).astype(BF)
            dup = (dact * silu).astype(BF)
            gs[slot][:, f : f + half] = dgate
            gs[slot][:, fc + f : fc + f + half] = dup
            g[c, rows, f : f + half] = dgate
            g[c, rows, fc + f : fc + f + half] = dup

        def down_grad(i, slot):
            rows = aligned(i % TILES * tm, tm)
            acc[2] += dot_tn(acts[slot][...], y[rows, :])

        def in_grads(i, slot):
            rows = aligned(i % TILES * tm, tm)
            at = a[l, rows, :]
            acc[0] += dot_tn(at, gs[slot][:, :fc])
            acc[1] += dot_tn(at, gs[slot][:, fc:])

        @pl.when(turn == 0)
        def _():
            for m in range(3):
                arrived(items // layers * (layers - 1) + m)

        for f in (0, half):
            grads_in(0, 0, f)

        def body(j, _):
            @pl.when((turn == 0) & (last + j < items + done))
            def _():
                gather(last + j)

            @pl.when((turn == 0) & (j % per == per - 1) & (j < (chunks - 1) * per))
            def _():
                for m in range(3):
                    arrived(items // layers * (layers - 1) + 3 * (j // per + 1) + m)

            reduce(turn, j)
            for k in range(2):
                i = 2 * j + k
                ahead = jnp.minimum(i + 1, chunks * TILES - 1)
                grads_in(ahead, (k + 1) % 2, 0)
                down_grad(i, k % 2)
                grads_in(ahead, (k + 1) % 2, half)
                in_grads(i, k % 2)
            return 0

        def chunk(c, _):
            lax.fori_loop(c * per, (c + 1) * per, body, 0)
            for m in range(3):
                terms[c, m] = acc[m].astype(BF)
                acc[m] = jnp.zeros_like(acc[m])
            return 0

        lax.fori_loop(0, chunks, chunk, 0)

        def fetch(j):
            @pl.when(l == 0)
            def _():
                io_in(x_hbm, j).start()

            @pl.when(l != 0)
            def _():
                io_in(h_hbm, j).start()

        fetch(0)

        def inputs(j, _):
            reduce(turn, chunks * per + j)
            io_in(x_hbm, j).wait()

            @pl.when(j + 1 < per)
            def _():
                fetch(j + 1)

            for k in range(2):
                rows = aligned(j * big + k * tm, tm)
                da = sum(dot_nt(g[c, rows, m * fc : (m + 1) * fc], w[l, c, m]) for c in range(chunks) for m in range(2))
                da = da.astype(BF).astype(F32)
                wide = io[j % 2, pl.ds(k * tm, tm), :].astype(F32)
                scale = scale_of(wide)
                along = jnp.mean(da * wide, -1, keepdims=True) * (scale * scale * scale)
                dh = (da * scale - wide * along).astype(BF).astype(F32)
                y[rows, :] = (y[rows, :].astype(F32) + dh).astype(BF)

            @pl.when(l == 0)
            def _():
                rows = aligned(j * big, big)
                pltpu.make_async_copy(y.at[rows, :], dx_hbm.at[rows, :], sem.at[0]).start()

            return 0

        lax.fori_loop(0, per, inputs, 0)
        return 0

    lax.fori_loop(0, layers, backward, 0)

    def tail(q, _):
        reduce(layers - 1, q)
        return 0

    lax.fori_loop((chunks + 1) * per, (chunks + 1) * per + 3 * (near + 1) + 3 - per, tail, 0)
    for p in range(chunks):
        down_out(0, p).wait()
    for m in range(2):
        for j in range(3):
            in_out(0, m, j).wait()
    pltpu.make_async_copy(y, dx_hbm, sem.at[0]).wait()

    def sent(i, _):
        ref = w.at[0, 0, 0, pl.ds(0, (n - 1) * own), :]
        pltpu.make_async_copy(ref, ref, ag_send.at[i]).wait()
        return 0

    lax.fori_loop(0, items, sent, 0)


def layers_of(n, x, dy, gate, up, down):
    tokens, d = x.shape
    layers, own, ff = gate.shape
    fc = ff // CHUNKS
    tm = tokens // TILES
    items = layers * CHUNKS * 3
    assert d == fc == n * own and down.shape == (layers, CHUNKS * own, d) and own == 64 and n % 2 == 0
    assert (TILES // 2) % 3 == 2 and layers > 1
    hbm = pl.BlockSpec(memory_space=pl.ANY)
    dma = pltpu.SemaphoreType.DMA
    near = (n - 1) // 2
    return pl.pallas_call(
        functools.partial(kernel, n),
        out_shape=[jax.ShapeDtypeStruct(t.shape, BF) for t in (x, gate, up, down, x)],
        in_specs=[hbm] * 5,
        out_specs=[hbm] * 5,
        scratch_shapes=[
            pltpu.VMEM((layers, tokens, d), BF),
            pltpu.VMEM((tokens, d), BF),
            pltpu.VMEM((CHUNKS, tokens, 2 * fc), BF),
            pltpu.VMEM((layers, CHUNKS, 3, d, fc), BF),
            pltpu.VMEM((3, d, fc), F32),
            pltpu.VMEM((tm, fc), BF),
            pltpu.VMEM((tm, fc), BF),
            pltpu.VMEM((tm, 2 * fc), BF),
            pltpu.VMEM((tm, 2 * fc), BF),
            pltpu.VMEM((CHUNKS, 3, d, fc), BF),
            pltpu.VMEM((CHUNKS, 3, n - 1, own, fc), BF),
            pltpu.VMEM((CHUNKS, 3, own, fc), BF),
            pltpu.VMEM((2, CHUNKS, own, fc), BF),
            pltpu.VMEM((2, 2 * tm, d), BF),
            dma((2 + layers * 9,)),
            dma((2, 2)),
            dma((CHUNKS * 3,)),
            dma((items, n - 1)),
            dma((items,)),
            dma((items,)),
            dma((CHUNKS, 3, n - 1)),
            dma((CHUNKS, 3)),
            pltpu.SemaphoreType.REGULAR((2, CHUNKS, 3)),
        ],
        compiler_params=pltpu.CompilerParams(vmem_limit_bytes=VMEM_LIMIT, has_side_effects=True, collective_id=0),
        name="layers",
    )(x, dy, gate, up, down)


def solution(mesh):
    n = mesh.shape["dp"]
    assert mesh.shape["rep"] % 2 == 0

    def local(x, dy, gate, up, down):
        dx, dgate, dup, ddown, _ = layers_of(n, x[0], dy[0], gate, up, down)
        return dx[None], dgate, dup, ddown

    both, rows = P(("rep", "dp"), None, None), P(None, "dp", None)
    grads = P("rep", "dp", None)
    return jax.shard_map(
        local, mesh=mesh, in_specs=(both, both, rows, rows, rows), out_specs=(both, grads, grads, grads), check_vma=False
    )
```

time: 541 us -> 229 us (0.42)
  waiting for transfers between devices: 278 us -> 0 us
  local copies, waits for them, and re-layouts: 83.4 us -> 6.81 us
  Pallas kernels: 159 us -> 220 us
  between operations: 14.5 us -> 0.67 us
    unnamed x6 -> x0, waiting for transfers between devices: 138 us -> none
    all_gather x3 -> x0, waiting for transfers between devices: 98.6 us -> none  [the longest x2 73.7 us: columns(): t = lax.all_gather(t, 'dp', axis=1, tiled=True)]
    pallas_call x1, Pallas kernels: 159 us -> 220 us  [layers_of(): pl.pallas_call(functools.partial(kernel, n), out_shape=[jax.ShapeDtypeStr...]
    reduce_scatter x1 -> x0, waiting for transfers between devices: 41.5 us -> none  [back_rows(): return lax.psum_scatter(t, 'dp', scatter_dimension=1, tiled=True)]
    reshape x3 -> x0, local copies, waits for them, and re-layouts: 20 us -> none  [the longest x2 17.6 us: back_columns(): t.reshape(layers, CHUNKS, d, n, own).transpose(0, 2, 3, 1, 4)]
    all_gather x2 -> x0, local copies, waits for them, and re-layouts: 15.6 us -> none  [columns(): t = lax.all_gather(t, 'dp', axis=1, tiled=True)]
    transpose x5 -> x0, local copies, waits for them, and re-layouts: 15.6 us -> none  [the longest x2 7.87 us: back_columns(): t.reshape(layers, CHUNKS, d, n, own).transpose(0, 2, 3, 1, 4)]
    slice x3 -> x0, local copies, waits for them, and re-layouts: 15.3 us -> none  [the longest x1 5.92 us: local(): terms[:, :, 2]]
  transfers between devices with their start and end apart: 5 -> 0, of which waited for: 5 -> 0; matrix products, arithmetic and copies ran while one was open for 7% -> 0% of each run, Pallas kernels for 0% -> 0%
where the time goes in v2:
time: 229 us; the launch traced here: 227 us
  Pallas kernels  220 us (96%)
  local copies, waits for them, and re-layouts  6.81 us (3%)
    pallas_call x1, Pallas kernels, layers_of(): pl.pallas_call(functools.partial(kernel, n), out_shape=[jax.ShapeDtypeStr...  220 us
    unnamed x10, local copies, waits for them, and re-layouts  6.81 us

profile of v2, /device:TPU:22, one launch (start us, length us, event | category | flops | bytes accessed | tf_op | source)
XLA Modules:
  0.0 227.5 jit_solution(16175417924522370606)
XLA Ops:
  0.6 220.0 %layers.1 = (bf16[4096,512]{1,0:T(8,128)(2,1)}, bf16[2,64,1536]{2,1,0:T(8,128)(2,1)}, bf16[2,64,1536]{2,1,0:T(8,128)(2,1)}, bf16[2,192,512]{2,1,0:T(8,128)(2,1)}, bf16[4096,512]{1,0:T(8,128)(2,1)}) custom-call(bf16[4096,512]{1,0:T(8,128)(2,1)} %bitcast.3, bf16[4096,512]{1,0:T(8,128)(2,1)} %bitcast.4, bf16[2,64,1536]{2,1,0:T(8,128)(2,1)} %gate_hbm.1, ...), custom_call_target="tpu_custom_call" | custom-call | tf_op jit(solution)/shard_map/layers/pallas_call | solution.py:478
  220.7 0.0 copy-start.2
  220.7 0.0 copy-start.1
  220.7 0.0 copy-start
  220.7 4.6 %copy.13 = bf16[1,4096,512]{2,1,0:T(8,128)(2,1)} copy(bf16[1,4096,512]{2,1,0:T(8,128)(2,1)} %bitcast.5) | data formatting | bytes 8388608
  225.3 0.0 copy-done.2
  225.3 0.7 copy.14
  226.0 0.0 copy-done.1
  226.0 0.7 copy.15
  226.8 0.0 copy-done
  226.8 0.7 copy.16
Async XLA Ops:
  220.7 4.6 %copy-start.2 = (bf16[2,64,1536]{2,1,0:T(8,128)(2,1)S(1)}, bf16[2,64,1536]{2,1,0:T(8,128)(2,1)}, u32[]{:S(2)}) copy-start(bf16[2,64,1536]{2,1,0:T(8,128)(2,1)} %get-tuple-element.17) | copy-start | bytes 1179652
  220.7 5.3 %copy-start.1 = (bf16[2,64,1536]{2,1,0:T(8,128)(2,1)S(1)}, bf16[2,64,1536]{2,1,0:T(8,128)(2,1)}, u32[]{:S(2)}) copy-start(bf16[2,64,1536]{2,1,0:T(8,128)(2,1)} %get-tuple-element.18) | copy-start | bytes 1179652
  220.7 6.1 %copy-start = (bf16[2,192,512]{2,1,0:T(8,128)(2,1)S(1)}, bf16[2,192,512]{2,1,0:T(8,128)(2,1)}, u32[]{:S(2)}) copy-start(bf16[2,192,512]{2,1,0:T(8,128)(2,1)} %get-tuple-element.19) | copy-start | bytes 1179652

commit v3 on v0

v3 whole, which is shorter than its diff:
```python
import functools

import jax
import jax.numpy as jnp
from jax import lax
from jax.experimental import pallas as pl
from jax.experimental.pallas import tpu as pltpu
from jax.sharding import PartitionSpec as P

BF = jnp.bfloat16
F32 = jnp.float32
CHUNKS = 3
TILES = 16
BODIES = TILES // 2

GATHER_START = (
    ((0, 0), (1, 0)),
    ((0, 1), (1, 1), (2, 0), (3, 0)),
    ((0, 2), (1, 2), (2, 1), (3, 1)),
    ((0, 3), (1, 3), (2, 2), (3, 2), (4, 0), (5, 0)),
    ((0, 4), (1, 4), (2, 3), (3, 3)),
)
GATHER_HIDDEN = {
    1: ((2, 4), (3, 4), (4, 1), (5, 1), (6, 0)),
    5: ((4, 2), (5, 2)),
    9: ((4, 3), (5, 3), (6, 1)),
    13: ((4, 4), (5, 4), (7, 0)),
    14: ((6, 2),),
    18: ((6, 3), (7, 1)),
}
GATHER_DOWN = {0: ((6, 4), (7, 2)), 3: ((7, 3), (8, 0)), 6: ((7, 4),)}
GATHER_BACK = {0: ((8, 1),), 1: ((9, 0),), 2: ((8, 2),), 3: ((9, 1),), 4: ((8, 3),), 5: ((9, 2),), 6: ((8, 4),), 7: ((9, 3),), 9: ((9, 4),)}

SUMS_FIRST = [(BODIES * (p + 1) + 3 * s + u, p, u, s) for p in range(3) for s in range(5) for u in range(3)]
LATE = 4 * BODIES
SUMS_LEFT = [(1 + 4 * (s - 3) + u, 2, u, s) for s in (3, 4) for u in range(3)]
SUMS_SECOND = (
    [(8 + 4 * s + u, 0, u, s) for s in range(5) for u in range(3)]
    + [(17 + 4 * s + u, 1, u, s) for s in range(2) for u in range(3)]
    + [(25 + u, 1, u, 2) for u in range(3)] + [(28 + u, 1, u, 3) for u in range(3)] + [(31, 1, 0, 4), (31, 1, 1, 4), (32, 1, 2, 4)]
    + [(24, 2, 0, 0), (24, 2, 1, 0), (25, 2, 2, 0)] + [(27 + u, 2, u, 1) for u in range(3)] + [(30, 2, 0, 2), (31, 2, 1, 2), (31, 2, 2, 2)]
    + [(32, 2, u, s) for s in (3, 4) for u in range(3)]
)
EPS = 1e-6
VMEM_LIMIT = 67043328


def dot(a, b):
    return lax.dot_general(a, b, (((1,), (0,)), ((), ())), preferred_element_type=F32)


def dot_nt(a, b):
    return lax.dot_general(a, b, (((1,), (1,)), ((), ())), preferred_element_type=F32)


def dot_tn(a, b):
    return lax.dot_general(a, b, (((0,), (0,)), ((), ())), preferred_element_type=F32)


def sigmoid(g):
    return 0.5 * jnp.tanh(0.5 * g) + 0.5


def scale_of(wide):
    return lax.rsqrt(jnp.mean(wide * wide, -1, keepdims=True) + EPS)


def normed(wide):
    return (wide * scale_of(wide)).astype(BF)


def aligned(start, size):
    return pl.ds(pl.multiple_of(start, size), size)


def choose(j, table, do):
    keys = sorted(table)
    if len(keys) == 1:
        pl.when(j == keys[0])(lambda: do(table[keys[0]]))
    elif keys:
        mid = keys[len(keys) // 2]
        pl.when(j < mid)(lambda: choose(j, {k: v for k, v in table.items() if k < mid}, do))
        pl.when(j >= mid)(lambda: choose(j, {k: v for k, v in table.items() if k >= mid}, do))


def by_body(events, first, last):
    table = {}
    for at, *event in sorted(events, key=lambda e: (e[0], -e[3])):
        if first <= at < last:
            table.setdefault(at, []).append(event)
    return table


def kernel(
    n, x_hbm, dy_hbm, gate_hbm, up_hbm, down_hbm, dx_hbm, dgate_hbm, dup_hbm, ddown_hbm, h_hbm, gu_hbm,
    a1, y, g, w, acc, act0, act1, g0, g1, terms, slots, fin, io,
    sem, io_sem, gu_sem, out_sem, ag_recv, ag_send, side_recv, rs_recv, rs_send, credit,
):
    layers, chunks = w.shape[:2]
    tokens, d = y.shape
    fc = w.shape[-1]
    own = d // n
    half = fc // 2
    tm = tokens // TILES
    big = 2 * tm
    acts, gs = (act0, act1), (g0, g1)
    near = (n - 1) // 2

    me = lax.axis_index("dp")
    core = lax.axis_index("rep") % 2
    left, right = {"dp": (me + n - 1) % n}, {"dp": (me + 1) % n}
    partner = {"rep": lax.axis_index("rep") + 1 - 2 * core}
    owner = [(me + k) % n * own for k in range(n)]

    def remote(src, dst, send, recv, to):
        return pltpu.make_async_remote_copy(src, dst, send, recv, device_id=to, device_id_type=pl.DeviceIdType.MESH)

    ITEMS = [(0, c, m) for c in range(chunks) for m in range(2)] + [(0, slice(None), 2)] + [(l, c, slice(None)) for l in range(1, layers) for c in range(chunks)]

    def piece(i, rows):
        return w.at[(*ITEMS[i], rows, slice(None))]

    def gather(steps):
        for i, h in steps:
            far = near + i % 2
            for side, to in enumerate((right, left)):
                reach = (far, n - 1 - far)[side]
                if h > reach:
                    continue
                ref = piece(i, aligned(owner[(n - h) % n if side == 0 else h] + core * (own // 2), own // 2))
                at = side * far + h
                if h:
                    remote(ref, ref, ag_send.at[i], ag_recv.at[i, at - 1], to).wait_recv()
                if h < reach:
                    remote(ref, ref, ag_send.at[i], ag_recv.at[i, at], to).start()
                if h:
                    remote(ref, ref, ag_send.at[i], side_recv.at[i], partner).start()

    def arrived(*which):
        for i in which:
            ref = piece(i, pl.ds(0, (n - 1) * (own // 2)))
            pltpu.make_async_copy(ref, ref, side_recv.at[i]).wait()

    def reduce(turn, events):
        for p, u, s in events:
            far = near + (p + u) % 2
            for side, to in enumerate((right, left)):
                reach = (far, n - 1 - far)[side]
                if s >= reach:
                    continue
                at = side * far + s
                rows = aligned(owner[reach - s if side == 0 else n - reach + s], own)
                if s == 0:
                    if turn:
                        pl.semaphore_wait(credit.at[side, p, u], 1)
                    ref = terms.at[p, u, rows, :]
                else:
                    ref = slots.at[p, u, at - 1]
                    remote(ref, ref, rs_send.at[p, u], rs_recv.at[p, u, at - 1], to).wait_recv()
                    ref[...] = (ref[...].astype(F32) + terms[p, u, rows, :].astype(F32)).astype(BF)
                remote(ref, slots.at[p, u, at], rs_send.at[p, u], rs_recv.at[p, u, at], to).start()
            if s == near + 1:
                finish(turn, p, u, far)

    def down_out(l, p):
        return pltpu.make_async_copy(fin.at[p, 2], ddown_hbm.at[l, pl.ds(p * own, own), :], out_sem.at[p])

    def in_out(l, m, j):
        out = dgate_hbm if m == 0 else dup_hbm
        return pltpu.make_async_copy(fin.at[j, m], out.at[l, :, pl.ds(j * d, d)], out_sem.at[chunks + m * chunks + j])

    def finish(turn, p, u, far):
        l = layers - 1 - turn
        ends = [slots.at[p, u, far - 1], slots.at[p, u, n - 2]]
        for ref, at in zip(ends, (far - 1, n - 2)):
            remote(ref, ref, rs_send.at[p, u], rs_recv.at[p, u, at], right).wait_recv()
        if turn:
            (down_out(l + 1, p) if u == 2 else in_out(l + 1, u, p)).wait()
        rows = aligned(owner[0], own)
        fin[p, u] = (ends[0][...].astype(F32) + ends[1][...].astype(F32) + terms[p, u, rows, :].astype(F32)).astype(BF)
        ref = w.at[0, 0, 0, pl.ds(0, (n - 1) * own), :]
        pltpu.make_async_copy(ref, ref, rs_send.at[p, u]).wait()
        if l:
            pl.semaphore_signal(credit.at[0, p, u], 1, device_id=left, device_id_type=pl.DeviceIdType.MESH)
            pl.semaphore_signal(credit.at[1, p, u], 1, device_id=right, device_id_type=pl.DeviceIdType.MESH)
        if u == 2:
            down_out(l, p).start()
        if u < 2 and p == chunks - 1:
            low = lax.broadcasted_iota(jnp.int32, (own, 128), 1) < 64
            parts = [[fin[c, u, :, pl.ds(128 * e, 128)] for e in range(fc // 128)] for c in range(chunks)]
            for e in range(fc // 128):
                c0, c1, c2 = (parts[c][e].astype(F32) for c in range(chunks))
                c1 = pltpu.roll(c1, 64, 1)
                for k, (lo, hi) in enumerate(((c0, c1), (c2, c0), (c1, c2))):
                    j, at = divmod(3 * e + k, d // 128)
                    fin[j, u, :, pl.ds(128 * at, 128)] = jnp.where(low, lo, hi).astype(BF)
            for j in range(3):
                in_out(l, u, j).start()

    shards = (gate_hbm, up_hbm)
    raw = [
        pltpu.make_async_copy(shards[m].at[l, :, pl.ds(j * d, d)], terms.at[l, m, pl.ds(j * own, own), :], sem.at[2 + (l * 2 + m) * 3 + j])
        for l in range(layers) for m in range(2) for j in range(3)
    ]
    downs = [
        pltpu.make_async_copy(down_hbm.at[l, pl.ds(c * own, own), :], w.at[l, c, 2, aligned(owner[0], own), :], sem.at[2 + layers * 6 + l * 3 + c])
        for l in range(layers) for c in range(chunks)
    ]
    load_x, load_dy = pltpu.make_async_copy(x_hbm, a1, sem.at[0]), pltpu.make_async_copy(dy_hbm, y, sem.at[1])
    for copy in (*raw, *downs, load_x, load_dy):
        copy.start()
    barrier = pltpu.get_barrier_semaphore()
    for to in (left, right, partner):
        pl.semaphore_signal(barrier, 1, device_id=to, device_id_type=pl.DeviceIdType.MESH)
    for copy in (*raw, *downs):
        copy.wait()
    low = lax.broadcasted_iota(jnp.int32, (own, 128), 1) < 64
    for l in range(layers):
        for m in range(2):
            for e in range(fc // 128):
                parts = []
                for k in range(3):
                    j, at = divmod(3 * e + k, d // 128)
                    parts.append(terms[l, m, pl.ds(j * own, own), pl.ds(128 * at, 128)].astype(F32))
                k0, k1, k2 = parts
                mixed = (jnp.where(low, k0, k1), pltpu.roll(jnp.where(low, k2, k0), 64, 1), jnp.where(low, k1, k2))
                for c in range(chunks):
                    w[l, c, m, aligned(owner[0], own), pl.ds(128 * e, 128)] = mixed[c].astype(BF)
    pl.semaphore_wait(barrier, 3)

    gather(GATHER_START[0])
    load_x.wait()

    def norm_x(t, _):
        rows = aligned(t * tm, tm)
        a1[rows, :] = normed(a1[rows, :].astype(F32))
        return 0

    lax.fori_loop(0, TILES, norm_x, 0)
    for steps in GATHER_START[1:]:
        gather(steps)
    arrived(0, 1)

    def hidden_units(keep):
        def keep_out(b):
            return pltpu.make_async_copy(keep.at[b % 2], gu_hbm.at[pl.ds(2 * b, 2)], gu_sem.at[b % 2])

        def body(b, _):
            choose(b, GATHER_HIDDEN, gather)
            choose(b, {BODIES * c: (2 * c, 2 * c + 1) for c in range(1, chunks)}, lambda which: arrived(*which))
            pl.when(b >= 2)(lambda: keep_out(b - 2).wait())
            c = b // BODIES
            for k in range(2):
                rows = aligned(b % BODIES * big + k * tm, tm)
                at = a1[rows, :]
                for f in (0, half):
                    gate = dot(at, w[0, c, 0, :, f : f + half])
                    up = dot(at, w[0, c, 1, :, f : f + half])
                    keep[b % 2, k, 0, :, f : f + half] = gate
                    keep[b % 2, k, 1, :, f : f + half] = up
                    g[c, rows, f : f + half] = (gate * sigmoid(gate) * up).astype(BF)
            keep_out(b).start()
            return 0

        lax.fori_loop(0, chunks * BODIES, body, 0)
        for b in (chunks * BODIES - 2, chunks * BODIES - 1):
            keep_out(b).wait()

    def io_in(src, j):
        return pltpu.make_async_copy(src.at[aligned(j * big, big), :], io.at[j % 2], io_sem.at[0, j % 2])

    io_in(x_hbm, 0).start()
    io_in(x_hbm, 1).start()
    pl.run_scoped(hidden_units, pltpu.VMEM((2, 2, 2, tm, fc), F32))

    def backward(turn, a, gate_up, events):
        l = layers - 1 - turn
        tiles = chunks * TILES

        def grads_in(i, slot, f, kept):
            c, t = i // TILES, i % TILES
            rows = aligned(t * tm, tm)
            if kept is None:
                at = a[rows, :]
                gate = dot(at, w[l, c, 0, :, f : f + half])
                up = dot(at, w[l, c, 1, :, f : f + half])
            else:
                gate, up = kept[0, :, f : f + half], kept[1, :, f : f + half]
            dact = dot_nt(y[rows, :], w[l, c, 2, f : f + half, :]).astype(BF).astype(F32)
            s = sigmoid(gate)
            silu = gate * s
            acts[slot][:, f : f + half] = (silu * up).astype(BF)
            dgate = (dact * up * (s + silu * (1.0 - s))).astype(BF)
            dup = (dact * silu).astype(BF)
            gs[slot][:, f : f + half] = dgate
            gs[slot][:, fc + f : fc + f + half] = dup
            g[c, rows, f : f + half] = dgate
            g[c, rows, fc + f : fc + f + half] = dup

        def down_grad(i, slot):
            rows = aligned(i % TILES * tm, tm)
            acc[2] += dot_tn(acts[slot][...], y[rows, :])

        def in_grads(i, slot):
            rows = aligned(i % TILES * tm, tm)
            at = a[rows, :]
            acc[0] += dot_tn(at, gs[slot][:, :fc])
            acc[1] += dot_tn(at, gs[slot][:, fc:])

        def first_of(j):
            return jnp.minimum(2 * j + 1, tiles - 2)

        def block_in(j):
            return pltpu.make_async_copy(gu_hbm.at[pl.ds(first_of(j), 2)], gate_up.at[j % 3], gu_sem.at[j % 3])

        src = h_hbm if l else x_hbm
        io_in(src, 0).start()
        io_in(src, 1).start()
        if turn:
            first = pltpu.make_async_copy(gu_hbm.at[0], gate_up.at[2, 0], gu_sem.at[2])
            first.start()
            block_in(0).start()
            block_in(1).start()
            first.wait()
        for f in (0, half):
            grads_in(0, 0, f, gate_up.at[2, 0] if turn else None)

        def body(j, _):
            if not turn:
                choose(j, GATHER_BACK, gather)
                choose(j, {BODIES * c - 1: 3 * chunks - 2 + c for c in range(1, chunks)}, lambda i: arrived(i))
            choose(j, by_body(events, 0, chunks * BODIES), lambda e: run(turn, e))
            if turn:
                block_in(j).wait()
                pl.when(j + 2 < chunks * BODIES)(lambda: block_in(j + 2).start())
            for k in range(2):
                i = 2 * j + k
                ahead = jnp.minimum(i + 1, tiles - 1)
                kept = gate_up.at[j % 3, ahead - first_of(j) if k == 0 else 1] if turn else None
                grads_in(ahead, (k + 1) % 2, 0, kept)
                down_grad(i, k % 2)
                grads_in(ahead, (k + 1) % 2, half, kept)
                in_grads(i, k % 2)
            return 0

        def chunk(c, _):
            lax.fori_loop(c * BODIES, (c + 1) * BODIES, body, 0)
            for m in range(3):
                terms[c, m] = acc[m].astype(BF)
                acc[m] = jnp.zeros_like(acc[m])
            return 0

        lax.fori_loop(0, chunks, chunk, 0)

        def inputs(j, _):
            choose(j + chunks * BODIES, by_body(events, chunks * BODIES, LATE), lambda e: run(turn, e))
            io_in(src, j).wait()
            for k in range(2):
                rows = aligned(j * big + k * tm, tm)
                da = sum(dot_nt(g[c, rows, m * fc : (m + 1) * fc], w[l, c, m]) for c in range(chunks) for m in range(2))
                da = da.astype(BF).astype(F32)
                wide = io[j % 2, pl.ds(k * tm, tm), :].astype(F32)
                scale = scale_of(wide)
                along = jnp.mean(da * wide, -1, keepdims=True) * (scale * scale * scale)
                dh = (da * scale - wide * along).astype(BF).astype(F32)
                y[rows, :] = (y[rows, :].astype(F32) + dh).astype(BF)
            pl.when(j + 2 < BODIES)(lambda: io_in(src, j + 2).start())
            if l == 0:
                rows = aligned(j * big, big)
                pltpu.make_async_copy(y.at[rows, :], dx_hbm.at[rows, :], sem.at[0]).start()
            return 0

        lax.fori_loop(0, BODIES, inputs, 0)

    def run(turn, events):
        for *event, of in events:
            reduce(of, [event])

    for m in range(3):
        acc[m] = jnp.zeros_like(acc[m])

    def with_last(a2, out):
        def io_out(j):
            return pltpu.make_async_copy(out.at[j % 2], h_hbm.at[aligned(j * big, big), :], io_sem.at[1, j % 2])

        def down(j, _):
            choose(j, GATHER_DOWN, gather)
            pl.when(j == 0)(lambda: arrived(2 * chunks))
            io_in(x_hbm, j).wait()
            pl.when(j >= 2)(lambda: io_out(j - 2).wait())
            for k in range(2):
                rows = aligned(j * big + k * tm, tm)
                hidden = sum(dot(g[c, rows, :fc], w[0, c, 2]) for c in range(chunks))
                here = pl.ds(k * tm, tm)
                h = (io[j % 2, here, :].astype(F32) + hidden.astype(BF).astype(F32)).astype(BF)
                out[j % 2, here, :] = h
                a2[rows, :] = normed(h.astype(F32))
            io_out(j).start()
            pl.when(j + 2 < BODIES)(lambda: io_in(x_hbm, j + 2).start())
            return 0

        lax.fori_loop(0, BODIES, down, 0)
        io_out(BODIES - 2).wait()
        io_out(BODIES - 1).wait()
        load_dy.wait()
        arrived(2 * chunks + 1)
        backward(0, a2, None, [(*e, 0) for e in SUMS_FIRST if e[0] < LATE])

    pl.run_scoped(with_last, pltpu.VMEM((tokens, d), BF), pltpu.VMEM((2, big, d), BF))

    left_over = [(e[0] - LATE, *e[1:], 0) for e in SUMS_FIRST if e[0] >= LATE and e[3] < 3] + [(*e, 0) for e in SUMS_LEFT]
    second = left_over + [(*e, 1) for e in SUMS_SECOND]

    def with_first(gate_up):
        backward(1, a1, gate_up, second)

    pl.run_scoped(with_first, pltpu.VMEM((3, 2, 2, tm, fc), F32))

    for e in by_body(second, LATE, LATE + 1).values():
        run(1, sorted(e, key=lambda e: (e[2], e[0])))
    for p in range(chunks):
        down_out(0, p).wait()
    for m in range(2):
        for j in range(3):
            in_out(0, m, j).wait()
    pltpu.make_async_copy(y, dx_hbm, sem.at[0]).wait()
    for i in range(len(ITEMS)):
        ref = piece(i, pl.ds(0, (n - 1) * own))
        pltpu.make_async_copy(ref, ref, ag_send.at[i]).wait()


def layers_of(n, x, dy, gate, up, down):
    tokens, d = x.shape
    layers, own, ff = gate.shape
    fc = ff // CHUNKS
    tm = tokens // TILES
    items = 3 * CHUNKS + 1
    assert d == fc == n * own and down.shape == (layers, CHUNKS * own, d) and own == 64
    assert n == 8 and layers == 2
    hbm = pl.BlockSpec(memory_space=pl.ANY)
    dma = pltpu.SemaphoreType.DMA
    kept = jax.ShapeDtypeStruct((CHUNKS * TILES, 2, tm, fc), F32)
    return pl.pallas_call(
        functools.partial(kernel, n),
        out_shape=[*(jax.ShapeDtypeStruct(t.shape, BF) for t in (x, gate, up, down, x)), kept],
        in_specs=[hbm] * 5,
        out_specs=[hbm] * 6,
        scratch_shapes=[
            pltpu.VMEM((tokens, d), BF),
            pltpu.VMEM((tokens, d), BF),
            pltpu.VMEM((CHUNKS, tokens, 2 * fc), BF),
            pltpu.VMEM((layers, CHUNKS, 3, d, fc), BF),
            pltpu.VMEM((3, d, fc), F32),
            pltpu.VMEM((tm, fc), BF),
            pltpu.VMEM((tm, fc), BF),
            pltpu.VMEM((tm, 2 * fc), BF),
            pltpu.VMEM((tm, 2 * fc), BF),
            pltpu.VMEM((CHUNKS, 3, d, fc), BF),
            pltpu.VMEM((CHUNKS, 3, n - 1, own, fc), BF),
            pltpu.VMEM((CHUNKS, 3, own, fc), BF),
            pltpu.VMEM((2, 2 * tm, d), BF),
            dma((2 + layers * 9,)),
            dma((2, 2)),
            dma((3,)),
            dma((CHUNKS * 3,)),
            dma((items, n - 1)),
            dma((items,)),
            dma((items,)),
            dma((CHUNKS, 3, n - 1)),
            dma((CHUNKS, 3)),
            pltpu.SemaphoreType.REGULAR((2, CHUNKS, 3)),
        ],
        compiler_params=pltpu.CompilerParams(vmem_limit_bytes=VMEM_LIMIT, has_side_effects=True, collective_id=0),
        name="layers",
    )(x, dy, gate, up, down)[:4]


def copied(*arrays):
    parts = [t.reshape(-1, t.shape[-1]) for t in arrays]
    cuts = [8, *(1 for _ in parts[1:])]

    def kernel(*refs):
        k = len(parts)
        src, dst, bufs, sems = refs[:k], refs[k : 2 * k], refs[2 * k : 3 * k], refs[3 * k]
        moves = []
        for which, (s, t, buf, cut) in enumerate(zip(src, dst, bufs, cuts)):
            size = s.shape[0] // cut
            for j in range(cut):
                rows = pl.ds(j * size, size)
                at = sems.at[:, 8 * which + j]
                moves.append((pltpu.make_async_copy(s.at[rows], buf.at[rows], at.at[0]), pltpu.make_async_copy(buf.at[rows], t.at[rows], at.at[1])))
        for there, _ in moves:
            there.start()
        for there, back in moves:
            there.wait()
            back.start()
        for _, back in moves:
            back.wait()

    hbm = pl.BlockSpec(memory_space=pl.ANY)
    out = pl.pallas_call(
        kernel,
        out_shape=[jax.ShapeDtypeStruct(t.shape, t.dtype) for t in parts],
        in_specs=[hbm] * len(parts),
        out_specs=[hbm] * len(parts),
        scratch_shapes=[*(pltpu.VMEM(t.shape, t.dtype) for t in parts), pltpu.SemaphoreType.DMA((2, 8 * len(parts)))],
        name="outputs",
    )(*parts)
    return [t.reshape(like.shape) for t, like in zip(out, arrays)]


def solution(mesh):
    n = mesh.shape["dp"]
    assert mesh.shape["rep"] % 2 == 0

    def local(x, dy, gate, up, down):
        dx, *grads = copied(*layers_of(n, x[0], dy[0], gate, up, down))
        return dx[None], *grads

    both, rows = P(("rep", "dp"), None, None), P(None, "dp", None)
    grads = P("rep", "dp", None)
    return jax.shard_map(
        local, mesh=mesh, in_specs=(both, both, rows, rows, rows), out_specs=(both, grads, grads, grads), check_vma=False
    )
```

time: 760 us -> 208 us (0.27)
  matrix products: 325 us -> 0 us
  Pallas kernels: 0 us -> 207 us
  waiting for transfers between devices: 145 us -> 0 us
  starting transfers between devices: 88.2 us -> 0 us
  local copies, waits for them, and re-layouts: 82.6 us -> 0 us
  other arithmetic: 72.6 us -> 0 us
  loops' own time: 25.5 us -> 0 us
  between operations: 14.8 us -> 0.8 us
    dot_general x35 -> x0, matrix products: 325 us -> none  [the longest x12 126 us: layer(): gate = jnp.dot(a, w['w_gate'], preferred_element_type=jnp.float32)]
    pallas_call x0 -> x2, Pallas kernels: none -> 207 us  [the longest x1 202 us: layers_of(): pl.pallas_call(functools.partial(kernel, n), out_shape=[*(jax.ShapeDtypeS...]
    squeeze x6 -> x0, waiting for transfers between devices: 95.4 us -> none  [stack(): h = layer(h, {name: w[number] for name, w in weights.items()})]
    dot_general x54 -> x0, starting transfers between devices: 87.8 us -> none  [the longest x18 33 us: layer(): gate = jnp.dot(a, w['w_gate'], preferred_element_type=jnp.float32)]
    unnamed x71 -> x0, local copies, waits for them, and re-layouts: 67.8 us -> none
    dot_general x54 -> x0, waiting for transfers between devices: 47.5 us -> none  [the longest x18 29.8 us: matmul(): jnp.dot(a, w, preferred_element_type=jnp.float32).astype(jnp.bfloat16)]
    convert_element_type x2 -> x0, other arithmetic: 35.4 us -> none  [the longest x1 32.6 us: layer(): (jax.nn.silu(gate) * up).astype(jnp.bfloat16)]
    another operation x6 -> x0, loops' own time: 25.5 us -> none  [the longest x2 8.76 us: layer(): up = jnp.dot(a, w['w_up'], preferred_element_type=jnp.float32)]
  transfers between devices with their start and end apart: 60 -> 0, of which waited for: 21 -> 0; matrix products, arithmetic and copies ran while one was open for 51% -> 0% of each run, Pallas kernels for 0% -> 0%
where the time goes in v3:
time: 208 us
  Pallas kernels  207 us (100%)
    pallas_call x1, Pallas kernels, layers_of(): pl.pallas_call(functools.partial(kernel, n), out_shape=[*(jax.ShapeDtypeS...  202 us
    pallas_call x1, Pallas kernels, copied(): pl.pallas_call(kernel, out_shape=[jax.ShapeDtypeStruct(t.shape, t.dtype)...  5.18 us

profile of v3, /device:TPU:22, one launch (start us, length us, event | category | flops | bytes accessed | tf_op | source)
XLA Modules:
  0.0 207.7 jit_solution(632996018768463958)
XLA Ops:
  0.6 201.7 %layers.1 = (bf16[4096,512]{1,0:T(8,128)(2,1)}, bf16[2,64,1536]{2,1,0:T(8,128)(2,1)}, bf16[2,64,1536]{2,1,0:T(8,128)(2,1)}, bf16[2,192,512]{2,1,0:T(8,128)(2,1)}...) custom-call(bf16[4096,512]{1,0:T(8,128)(2,1)} %bitcast.9, bf16[4096,512]{1,0:T(8,128)(2,1)} %bitcast.10, ...), custom_call_target="tpu_custom_call" | custom-call | tf_op jit(solution)/shard_map/layers/pallas_call | solution.py:443
  202.4 5.2 %outputs.1 = (bf16[4096,512]{1,0:T(8,128)(2,1)}, bf16[128,1536]{1,0:T(8,128)(2,1)}, bf16[128,1536]{1,0:T(8,128)(2,1)}, bf16[384,512]{1,0:T(8,128)(2,1)}) custom-call(bf16[4096,512]{1,0:T(8,128)(2,1)} %get-tuple-element.12.refs_0_, bf16[128,1536]{1,0:T(8,128)(2,1)} %bitcast.11, bf16[128,1536]{1,0:T(8,128)(2,1)} %bitcast.12, bf16[384,512]{1,0:T(8,128)(2,1)} %bitcast.13), custom_call_target="tpu_custom_call" | custom-call | tf_op jit(solution)/shard_map/outputs/pallas_call | solution.py:501

commit v4 on v3

--- a/solution.py
+++ b/solution.py
@@ -14,22 +14,18 @@
 BODIES = TILES // 2
 
 GATHER_START = (
-    ((0, 0), (1, 0)),
-    ((0, 1), (1, 1), (2, 0), (3, 0)),
-    ((0, 2), (1, 2), (2, 1), (3, 1)),
-    ((0, 3), (1, 3), (2, 2), (3, 2), (4, 0), (5, 0)),
+    ((0, 0), (1, 0), (2, 0), (3, 0), (4, 0), (5, 0)),
+    ((0, 1), (1, 1), (3, 1), (4, 1), (5, 1)),
+    ((0, 2), (1, 2), (2, 1), (6, 0)),
+    ((0, 3), (1, 3), (2, 2), (3, 2), (5, 2), (6, 1)),
     ((0, 4), (1, 4), (2, 3), (3, 3)),
 )
 GATHER_HIDDEN = {
-    1: ((2, 4), (3, 4), (4, 1), (5, 1), (6, 0)),
-    5: ((4, 2), (5, 2)),
-    9: ((4, 3), (5, 3), (6, 1)),
-    13: ((4, 4), (5, 4), (7, 0)),
-    14: ((6, 2),),
-    18: ((6, 3), (7, 1)),
+    0: ((4, 2),), 2: ((7, 0),), 4: ((6, 2),), 5: ((3, 4), (5, 3)), 6: ((2, 4),), 7: ((4, 3),), 8: ((7, 1),), 11: ((6, 3), (8, 0)),
+    12: ((9, 0),), 13: ((5, 4),), 14: ((4, 4),), 16: ((7, 2),), 21: ((6, 4), (8, 1)), 22: ((9, 1),),
 }
-GATHER_DOWN = {0: ((6, 4), (7, 2)), 3: ((7, 3), (8, 0)), 6: ((7, 4),)}
-GATHER_BACK = {0: ((8, 1),), 1: ((9, 0),), 2: ((8, 2),), 3: ((9, 1),), 4: ((8, 3),), 5: ((9, 2),), 6: ((8, 4),), 7: ((9, 3),), 9: ((9, 4),)}
+GATHER_DOWN = {1: ((7, 3),), 4: ((8, 2),), 6: ((7, 4),), 7: ((9, 2),)}
+GATHER_BACK = {1: ((8, 3),), 3: ((9, 3),), 5: ((8, 4),), 11: ((9, 4),)}
 
 SUMS_FIRST = [(BODIES * (p + 1) + 3 * s + u, p, u, s) for p in range(3) for s in range(5) for u in range(3)]
 LATE = 4 * BODIES
@@ -243,12 +239,12 @@
 
     def hidden_units(keep):
         def keep_out(b):
-            return pltpu.make_async_copy(keep.at[b % 2], gu_hbm.at[pl.ds(2 * b, 2)], gu_sem.at[b % 2])
+            return pltpu.make_async_copy(keep.at[b % 3], gu_hbm.at[pl.ds(2 * b, 2)], gu_sem.at[b % 3])
 
         def body(b, _):
             choose(b, GATHER_HIDDEN, gather)
             choose(b, {BODIES * c: (2 * c, 2 * c + 1) for c in range(1, chunks)}, lambda which: arrived(*which))
-            pl.when(b >= 2)(lambda: keep_out(b - 2).wait())
+            pl.when(b >= 3)(lambda: keep_out(b - 3).wait())
             c = b // BODIES
             for k in range(2):
                 rows = aligned(b % BODIES * big + k * tm, tm)
@@ -256,14 +252,14 @@
                 for f in (0, half):
                     gate = dot(at, w[0, c, 0, :, f : f + half])
                     up = dot(at, w[0, c, 1, :, f : f + half])
-                    keep[b % 2, k, 0, :, f : f + half] = gate
-                    keep[b % 2, k, 1, :, f : f + half] = up
+                    keep[b % 3, k, 0, :, f : f + half] = gate
+                    keep[b % 3, k, 1, :, f : f + half] = up
                     g[c, rows, f : f + half] = (gate * sigmoid(gate) * up).astype(BF)
             keep_out(b).start()
             return 0
 
         lax.fori_loop(0, chunks * BODIES, body, 0)
-        for b in (chunks * BODIES - 2, chunks * BODIES - 1):
+        for b in range(chunks * BODIES - 3, chunks * BODIES):
             keep_out(b).wait()
 
     def io_in(src, j):
@@ -271,9 +267,9 @@
 
     io_in(x_hbm, 0).start()
     io_in(x_hbm, 1).start()
-    pl.run_scoped(hidden_units, pltpu.VMEM((2, 2, 2, tm, fc), F32))
-
-    def backward(turn, a, gate_up, events):
+    pl.run_scoped(hidden_units, pltpu.VMEM((3, 2, 2, tm, fc), F32))
+
+    def backward(turn, a, gate_up, events, pending):
         l = layers - 1 - turn
         tiles = chunks * TILES
 
@@ -317,13 +313,14 @@
         io_in(src, 0).start()
         io_in(src, 1).start()
         if turn:
-            first = pltpu.make_async_copy(gu_hbm.at[0], gate_up.at[2, 0], gu_sem.at[2])
-            first.start()
+            for copy in first_tile:
+                copy.wait()
             block_in(0).start()
             block_in(1).start()
-            first.wait()
         for f in (0, half):
-            grads_in(0, 0, f, gate_up.at[2, 0] if turn else None)
+            grads_in(0, 0, f, acc.at[0, pl.ds(0, 2 * tm), :].reshape(2, tm, fc) if turn else None)
+        if turn:
+            acc[0] = jnp.zeros_like(acc[0])
 
         def body(j, _):
             if not turn:
@@ -351,6 +348,10 @@
             return 0
 
         lax.fori_loop(0, chunks, chunk, 0)
+        for copy in pending:
+            copy.wait()
+        for copy in first_tile if not turn else ():
+            copy.start()
 
         def inputs(j, _):
             choose(j + chunks * BODIES, by_body(events, chunks * BODIES, LATE), lambda e: run(turn, e))
@@ -378,6 +379,7 @@
 
     for m in range(3):
         acc[m] = jnp.zeros_like(acc[m])
+    first_tile = [pltpu.make_async_copy(gu_hbm.at[0, m], acc.at[0, pl.ds(m * tm, tm), :], gu_sem.at[m]) for m in range(2)]
 
     def with_last(a2, out):
         def io_out(j):
@@ -400,11 +402,9 @@
             return 0
 
         lax.fori_loop(0, BODIES, down, 0)
-        io_out(BODIES - 2).wait()
-        io_out(BODIES - 1).wait()
         load_dy.wait()
         arrived(2 * chunks + 1)
-        backward(0, a2, None, [(*e, 0) for e in SUMS_FIRST if e[0] < LATE])
+        backward(0, a2, None, [(*e, 0) for e in SUMS_FIRST if e[0] < LATE], [io_out(BODIES - 2), io_out(BODIES - 1)])
 
     pl.run_scoped(with_last, pltpu.VMEM((tokens, d), BF), pltpu.VMEM((2, big, d), BF))
 
@@ -412,7 +412,7 @@
     second = left_over + [(*e, 1) for e in SUMS_SECOND]
 
     def with_first(gate_up):
-        backward(1, a1, gate_up, second)
+        backward(1, a1, gate_up, second, ())
 
     pl.run_scoped(with_first, pltpu.VMEM((3, 2, 2, tm, fc), F32))
 

time: 208 us -> 198 us (0.952)
  Pallas kernels: 207 us -> 197 us
    pallas_call x1, Pallas kernels: 202 us -> 192 us  [layers_of(): pl.pallas_call(functools.partial(kernel, n), out_shape=[*(jax.ShapeDtypeS...]
where the time goes in v4:
time: 198 us
  Pallas kernels  197 us (99%)
    pallas_call x1, Pallas kernels, layers_of(): pl.pallas_call(functools.partial(kernel, n), out_shape=[*(jax.ShapeDtypeS...  192 us
    pallas_call x1, Pallas kernels, copied(): pl.pallas_call(kernel, out_shape=[jax.ShapeDtypeStruct(t.shape, t.dtype)...  5.18 us

profile of v4, /device:TPU:22, one launch (start us, length us, event | category | flops | bytes accessed | tf_op | source)
XLA Modules:
  0.0 197.6 jit_solution(7322453908412691476)
XLA Ops:
  0.6 191.6 %layers.1 = (bf16[4096,512]{1,0:T(8,128)(2,1)}, bf16[2,64,1536]{2,1,0:T(8,128)(2,1)}, bf16[2,64,1536]{2,1,0:T(8,128)(2,1)}, bf16[2,192,512]{2,1,0:T(8,128)(2,1)}...) custom-call(bf16[4096,512]{1,0:T(8,128)(2,1)} %bitcast.9, bf16[4096,512]{1,0:T(8,128)(2,1)} %bitcast.10, ...), custom_call_target="tpu_custom_call" | custom-call | tf_op jit(solution)/shard_map/layers/pallas_call | solution.py:443
  192.2 5.2 %outputs.1 = (bf16[4096,512]{1,0:T(8,128)(2,1)}, bf16[128,1536]{1,0:T(8,128)(2,1)}, bf16[128,1536]{1,0:T(8,128)(2,1)}, bf16[384,512]{1,0:T(8,128)(2,1)}) custom-call(bf16[4096,512]{1,0:T(8,128)(2,1)} %get-tuple-element.12.refs_0_, bf16[128,1536]{1,0:T(8,128)(2,1)} %bitcast.11, bf16[128,1536]{1,0:T(8,128)(2,1)} %bitcast.12, bf16[384,512]{1,0:T(8,128)(2,1)} %bitcast.13), custom_call_target="tpu_custom_call" | custom-call | tf_op jit(solution)/shard_map/outputs/pallas_call | solution.py:501

commit v5 on v4

--- a/solution.py
+++ b/solution.py
@@ -25,18 +25,24 @@
     12: ((9, 0),), 13: ((5, 4),), 14: ((4, 4),), 16: ((7, 2),), 21: ((6, 4), (8, 1)), 22: ((9, 1),),
 }
 GATHER_DOWN = {1: ((7, 3),), 4: ((8, 2),), 6: ((7, 4),), 7: ((9, 2),)}
-GATHER_BACK = {1: ((8, 3),), 3: ((9, 3),), 5: ((8, 4),), 11: ((9, 4),)}
-
-SUMS_FIRST = [(BODIES * (p + 1) + 3 * s + u, p, u, s) for p in range(3) for s in range(5) for u in range(3)]
-LATE = 4 * BODIES
-SUMS_LEFT = [(1 + 4 * (s - 3) + u, 2, u, s) for s in (3, 4) for u in range(3)]
-SUMS_SECOND = (
-    [(8 + 4 * s + u, 0, u, s) for s in range(5) for u in range(3)]
-    + [(17 + 4 * s + u, 1, u, s) for s in range(2) for u in range(3)]
-    + [(25 + u, 1, u, 2) for u in range(3)] + [(28 + u, 1, u, 3) for u in range(3)] + [(31, 1, 0, 4), (31, 1, 1, 4), (32, 1, 2, 4)]
-    + [(24, 2, 0, 0), (24, 2, 1, 0), (25, 2, 2, 0)] + [(27 + u, 2, u, 1) for u in range(3)] + [(30, 2, 0, 2), (31, 2, 1, 2), (31, 2, 2, 2)]
-    + [(32, 2, u, s) for s in (3, 4) for u in range(3)]
-)
+GATHER_BACK = {0: ((8, 3),), 2: ((8, 4), (9, 3)), 4: ((9, 4),)}
+WIDTHS = (4, 2)
+
+SUMS = {
+    4: ((0, 0, 0, 0),), 6: ((0, 0, 1, 0), (0, 0, 2, 0),), 7: ((0, 0, 0, 1),), 8: ((0, 1, 0, 0), (0, 1, 2, 0),),
+    10: ((0, 0, 1, 1), (0, 0, 2, 1), (0, 1, 0, 1), (0, 1, 2, 1),), 11: ((0, 1, 1, 0),), 12: ((0, 0, 1, 2), (0, 0, 2, 2),), 13: ((0, 2, 1, 0),),
+    14: ((0, 1, 1, 1), (0, 2, 0, 0), (0, 2, 2, 0),), 15: ((0, 0, 2, 3), (0, 0, 0, 2), (0, 1, 2, 2),), 16: ((0, 1, 0, 2), (0, 2, 1, 1),),
+    18: ((0, 0, 2, 4), (0, 2, 0, 1),), 19: ((0, 2, 2, 1),), 20: ((0, 0, 0, 3),), 21: ((0, 1, 1, 2),), 22: ((0, 1, 0, 3), (0, 2, 0, 2),),
+    23: ((0, 0, 0, 4), (0, 0, 1, 3), (0, 2, 1, 2), (0, 2, 2, 2),), 25: ((0, 1, 0, 4), (0, 1, 1, 3),), 26: ((0, 1, 2, 3),),
+    27: ((0, 0, 1, 4), (0, 2, 0, 3),), 28: ((0, 1, 1, 4), (1, 0, 2, 0),), 29: ((1, 0, 0, 0),), 30: ((0, 1, 2, 4), (0, 2, 0, 4), (1, 0, 1, 0),),
+    31: ((1, 0, 2, 1),), 32: ((1, 0, 0, 1),), 33: ((1, 0, 1, 1),), 34: ((0, 2, 2, 3), (1, 0, 2, 2),), 35: ((1, 0, 0, 2),),
+    36: ((1, 0, 1, 2), (1, 1, 0, 0),), 37: ((0, 2, 2, 4),), 38: ((0, 2, 1, 3), (1, 1, 1, 0), (1, 1, 2, 0),), 39: ((1, 0, 0, 3), (1, 0, 2, 3),),
+    40: ((1, 0, 1, 3),), 41: ((0, 2, 1, 4), (1, 1, 0, 1),), 42: ((1, 1, 1, 1),), 43: ((1, 0, 0, 4), (1, 1, 2, 1),),
+    44: ((1, 0, 1, 4), (1, 0, 2, 4), (1, 2, 0, 0), (1, 2, 1, 0),), 45: ((1, 1, 0, 2), (1, 2, 2, 0),), 46: ((1, 1, 2, 2),),
+    47: ((1, 2, 0, 1), (1, 2, 1, 1),), 48: ((1, 2, 2, 1),), 49: ((1, 1, 1, 2), (1, 2, 0, 2),), 50: ((1, 2, 1, 2), (1, 2, 2, 2),),
+    51: ((1, 1, 0, 3), (1, 1, 1, 3), (1, 1, 2, 3), (1, 2, 0, 3),),
+    52: ((1, 2, 1, 3), (1, 2, 2, 3), (1, 1, 0, 4), (1, 1, 1, 4), (1, 1, 2, 4), (1, 2, 0, 4), (1, 2, 1, 4), (1, 2, 2, 4),),
+}
 EPS = 1e-6
 VMEM_LIMIT = 67043328
 
@@ -77,14 +83,6 @@
         mid = keys[len(keys) // 2]
         pl.when(j < mid)(lambda: choose(j, {k: v for k, v in table.items() if k < mid}, do))
         pl.when(j >= mid)(lambda: choose(j, {k: v for k, v in table.items() if k >= mid}, do))
-
-
-def by_body(events, first, last):
-    table = {}
-    for at, *event in sorted(events, key=lambda e: (e[0], -e[3])):
-        if first <= at < last:
-            table.setdefault(at, []).append(event)
-    return table
 
 
 def kernel(
@@ -137,8 +135,8 @@
             ref = piece(i, pl.ds(0, (n - 1) * (own // 2)))
             pltpu.make_async_copy(ref, ref, side_recv.at[i]).wait()
 
-    def reduce(turn, events):
-        for p, u, s in events:
+    def reduce(events):
+        for turn, p, u, s in events:
             far = near + (p + u) % 2
             for side, to in enumerate((right, left)):
                 reach = (far, n - 1 - far)[side]
@@ -269,8 +267,12 @@
     io_in(x_hbm, 1).start()
     pl.run_scoped(hidden_units, pltpu.VMEM((3, 2, 2, tm, fc), F32))
 
-    def backward(turn, a, gate_up, events, pending):
+    def backward(turn, a, gate_up, start, pending):
         l = layers - 1 - turn
+        width = WIDTHS[turn]
+        bodies = TILES // width
+        table = {at - start: steps for at, steps in SUMS.items() if at >= start}
+        loop = chunks * bodies
         tiles = chunks * TILES
 
         def grads_in(i, slot, f, kept):
@@ -325,13 +327,13 @@
         def body(j, _):
             if not turn:
                 choose(j, GATHER_BACK, gather)
-                choose(j, {BODIES * c - 1: 3 * chunks - 2 + c for c in range(1, chunks)}, lambda i: arrived(i))
-            choose(j, by_body(events, 0, chunks * BODIES), lambda e: run(turn, e))
+                choose(j, {bodies * c - 1: 3 * chunks - 2 + c for c in range(1, chunks)}, lambda i: arrived(i))
+            choose(j, {at: steps for at, steps in table.items() if at < loop}, reduce)
             if turn:
                 block_in(j).wait()
-                pl.when(j + 2 < chunks * BODIES)(lambda: block_in(j + 2).start())
-            for k in range(2):
-                i = 2 * j + k
+                pl.when(j + 2 < loop)(lambda: block_in(j + 2).start())
+            for k in range(width):
+                i = width * j + k
                 ahead = jnp.minimum(i + 1, tiles - 1)
                 kept = gate_up.at[j % 3, ahead - first_of(j) if k == 0 else 1] if turn else None
                 grads_in(ahead, (k + 1) % 2, 0, kept)
@@ -341,7 +343,7 @@
             return 0
 
         def chunk(c, _):
-            lax.fori_loop(c * BODIES, (c + 1) * BODIES, body, 0)
+            lax.fori_loop(c * bodies, (c + 1) * bodies, body, 0)
             for m in range(3):
                 terms[c, m] = acc[m].astype(BF)
                 acc[m] = jnp.zeros_like(acc[m])
@@ -354,7 +356,7 @@
             copy.start()
 
         def inputs(j, _):
-            choose(j + chunks * BODIES, by_body(events, chunks * BODIES, LATE), lambda e: run(turn, e))
+            choose(j, {at - loop: steps for at, steps in table.items() if loop <= at < loop + BODIES}, reduce)
             io_in(src, j).wait()
             for k in range(2):
                 rows = aligned(j * big + k * tm, tm)
@@ -373,10 +375,6 @@
 
         lax.fori_loop(0, BODIES, inputs, 0)
 
-    def run(turn, events):
-        for *event, of in events:
-            reduce(of, [event])
-
     for m in range(3):
         acc[m] = jnp.zeros_like(acc[m])
     first_tile = [pltpu.make_async_copy(gu_hbm.at[0, m], acc.at[0, pl.ds(m * tm, tm), :], gu_sem.at[m]) for m in range(2)]
@@ -404,20 +402,16 @@
         lax.fori_loop(0, BODIES, down, 0)
         load_dy.wait()
         arrived(2 * chunks + 1)
-        backward(0, a2, None, [(*e, 0) for e in SUMS_FIRST if e[0] < LATE], [io_out(BODIES - 2), io_out(BODIES - 1)])
+        backward(0, a2, None, 0, [io_out(BODIES - 2), io_out(BODIES - 1)])
 
     pl.run_scoped(with_last, pltpu.VMEM((tokens, d), BF), pltpu.VMEM((2, big, d), BF))
 
-    left_over = [(e[0] - LATE, *e[1:], 0) for e in SUMS_FIRST if e[0] >= LATE and e[3] < 3] + [(*e, 0) for e in SUMS_LEFT]
-    second = left_over + [(*e, 1) for e in SUMS_SECOND]
-
     def with_first(gate_up):
-        backward(1, a1, gate_up, second, ())
+        backward(1, a1, gate_up, chunks * TILES // WIDTHS[0] + BODIES, ())
 
     pl.run_scoped(with_first, pltpu.VMEM((3, 2, 2, tm, fc), F32))
 
-    for e in by_body(second, LATE, LATE + 1).values():
-        run(1, sorted(e, key=lambda e: (e[2], e[0])))
+    reduce(SUMS[max(SUMS)])
     for p in range(chunks):
         down_out(0, p).wait()
     for m in range(2):

time: 198 us -> 193 us (0.975)
  Pallas kernels: 197 us -> 192 us
    pallas_call x1, Pallas kernels: 192 us -> 186 us  [layers_of(): pl.pallas_call(functools.partial(kernel, n), out_shape=[*(jax.ShapeDtypeS...]
where the time goes in v5:
time: 193 us; the launch traced here: 192 us
  Pallas kernels  192 us (99%)
    pallas_call x1, Pallas kernels, layers_of(): pl.pallas_call(functools.partial(kernel, n), out_shape=[*(jax.ShapeDtypeS...  186 us
    pallas_call x1, Pallas kernels, copied(): pl.pallas_call(kernel, out_shape=[jax.ShapeDtypeStruct(t.shape, t.dtype)...  5.18 us

profile of v5, /device:TPU:22, one launch (start us, length us, event | category | flops | bytes accessed | tf_op | source)
XLA Modules:
  0.0 192.3 jit_solution(6926693139811593190)
XLA Ops:
  0.6 186.3 %layers.1 = (bf16[4096,512]{1,0:T(8,128)(2,1)}, bf16[2,64,1536]{2,1,0:T(8,128)(2,1)}, bf16[2,64,1536]{2,1,0:T(8,128)(2,1)}, bf16[2,192,512]{2,1,0:T(8,128)(2,1)}...) custom-call(bf16[4096,512]{1,0:T(8,128)(2,1)} %bitcast.9, bf16[4096,512]{1,0:T(8,128)(2,1)} %bitcast.10, ...), custom_call_target="tpu_custom_call" | custom-call | tf_op jit(solution)/shard_map/layers/pallas_call | solution.py:437
  187.0 5.2 %outputs.1 = (bf16[4096,512]{1,0:T(8,128)(2,1)}, bf16[128,1536]{1,0:T(8,128)(2,1)}, bf16[128,1536]{1,0:T(8,128)(2,1)}, bf16[384,512]{1,0:T(8,128)(2,1)}) custom-call(bf16[4096,512]{1,0:T(8,128)(2,1)} %get-tuple-element.12.refs_0_, bf16[128,1536]{1,0:T(8,128)(2,1)} %bitcast.11, bf16[128,1536]{1,0:T(8,128)(2,1)} %bitcast.12, bf16[384,512]{1,0:T(8,128)(2,1)} %bitcast.13), custom_call_target="tpu_custom_call" | custom-call | tf_op jit(solution)/shard_map/outputs/pallas_call | solution.py:495

commit v6 on v5

--- a/solution.py
+++ b/solution.py
@@ -27,19 +27,20 @@
 GATHER_DOWN = {1: ((7, 3),), 4: ((8, 2),), 6: ((7, 4),), 7: ((9, 2),)}
 GATHER_BACK = {0: ((8, 3),), 2: ((8, 4), (9, 3)), 4: ((9, 4),)}
 WIDTHS = (4, 2)
+ORDERS = ((0, 1, 2, 3, 4), (1, 0, 2, 3, 4))
 
 SUMS = {
-    4: ((0, 0, 0, 0),), 6: ((0, 0, 1, 0), (0, 0, 2, 0),), 7: ((0, 0, 0, 1),), 8: ((0, 1, 0, 0), (0, 1, 2, 0),),
-    10: ((0, 0, 1, 1), (0, 0, 2, 1), (0, 1, 0, 1), (0, 1, 2, 1),), 11: ((0, 1, 1, 0),), 12: ((0, 0, 1, 2), (0, 0, 2, 2),), 13: ((0, 2, 1, 0),),
-    14: ((0, 1, 1, 1), (0, 2, 0, 0), (0, 2, 2, 0),), 15: ((0, 0, 2, 3), (0, 0, 0, 2), (0, 1, 2, 2),), 16: ((0, 1, 0, 2), (0, 2, 1, 1),),
-    18: ((0, 0, 2, 4), (0, 2, 0, 1),), 19: ((0, 2, 2, 1),), 20: ((0, 0, 0, 3),), 21: ((0, 1, 1, 2),), 22: ((0, 1, 0, 3), (0, 2, 0, 2),),
-    23: ((0, 0, 0, 4), (0, 0, 1, 3), (0, 2, 1, 2), (0, 2, 2, 2),), 25: ((0, 1, 0, 4), (0, 1, 1, 3),), 26: ((0, 1, 2, 3),),
-    27: ((0, 0, 1, 4), (0, 2, 0, 3),), 28: ((0, 1, 1, 4), (1, 0, 2, 0),), 29: ((1, 0, 0, 0),), 30: ((0, 1, 2, 4), (0, 2, 0, 4), (1, 0, 1, 0),),
-    31: ((1, 0, 2, 1),), 32: ((1, 0, 0, 1),), 33: ((1, 0, 1, 1),), 34: ((0, 2, 2, 3), (1, 0, 2, 2),), 35: ((1, 0, 0, 2),),
-    36: ((1, 0, 1, 2), (1, 1, 0, 0),), 37: ((0, 2, 2, 4),), 38: ((0, 2, 1, 3), (1, 1, 1, 0), (1, 1, 2, 0),), 39: ((1, 0, 0, 3), (1, 0, 2, 3),),
-    40: ((1, 0, 1, 3),), 41: ((0, 2, 1, 4), (1, 1, 0, 1),), 42: ((1, 1, 1, 1),), 43: ((1, 0, 0, 4), (1, 1, 2, 1),),
-    44: ((1, 0, 1, 4), (1, 0, 2, 4), (1, 2, 0, 0), (1, 2, 1, 0),), 45: ((1, 1, 0, 2), (1, 2, 2, 0),), 46: ((1, 1, 2, 2),),
-    47: ((1, 2, 0, 1), (1, 2, 1, 1),), 48: ((1, 2, 2, 1),), 49: ((1, 1, 1, 2), (1, 2, 0, 2),), 50: ((1, 2, 1, 2), (1, 2, 2, 2),),
+    4: ((0, 0, 0, 0), (0, 0, 1, 0), (0, 0, 2, 0),), 6: ((0, 0, 0, 1), (0, 0, 1, 1), (0, 0, 2, 1),),
+    8: ((0, 0, 1, 2), (0, 1, 0, 0), (0, 1, 1, 0), (0, 1, 2, 0),), 9: ((0, 0, 0, 2), (0, 0, 2, 2),), 10: ((0, 0, 1, 3), (0, 1, 0, 1), (0, 1, 1, 1),),
+    11: ((0, 0, 0, 3), (0, 1, 2, 1),), 12: ((0, 0, 1, 4), (0, 2, 0, 0), (0, 2, 1, 0), (0, 2, 2, 0),),
+    13: ((0, 0, 0, 4), (0, 0, 2, 3), (0, 1, 0, 2), (0, 1, 1, 2), (0, 1, 2, 2),), 14: ((0, 2, 0, 1),),
+    16: ((0, 0, 2, 4), (0, 1, 0, 3), (0, 2, 1, 1), (0, 2, 2, 1),), 18: ((0, 1, 1, 3), (0, 1, 2, 3),), 19: ((0, 1, 0, 4), (0, 2, 0, 2),),
+    20: ((0, 1, 1, 4), (0, 1, 2, 4), (0, 2, 1, 2), (0, 2, 2, 2),), 21: ((0, 2, 0, 3),), 25: ((0, 2, 0, 4),), 28: ((1, 0, 0, 0), (1, 0, 2, 0),),
+    29: ((1, 0, 1, 0),), 31: ((1, 0, 0, 1),), 32: ((1, 0, 2, 1),), 33: ((0, 2, 2, 3), (1, 0, 1, 1),), 34: ((0, 2, 1, 3), (1, 0, 0, 2),),
+    35: ((1, 0, 2, 2),), 36: ((0, 2, 2, 4), (1, 1, 0, 0), (1, 1, 2, 0),), 37: ((0, 2, 1, 4), (1, 0, 1, 2),), 38: ((1, 1, 1, 0),), 39: ((1, 0, 0, 3),),
+    40: ((1, 1, 0, 1),), 41: ((1, 1, 2, 1),), 42: ((1, 0, 1, 3), (1, 0, 2, 3), (1, 1, 1, 1),), 43: ((1, 0, 0, 4),),
+    44: ((1, 2, 0, 0), (1, 2, 1, 0), (1, 2, 2, 0),), 45: ((1, 0, 1, 4), (1, 0, 2, 4), (1, 1, 0, 2),), 46: ((1, 2, 0, 1),),
+    47: ((1, 2, 1, 1), (1, 2, 2, 1),), 48: ((1, 1, 1, 2), (1, 1, 2, 2), (1, 2, 0, 2),), 49: ((1, 2, 1, 2),), 50: ((1, 2, 2, 2),),
     51: ((1, 1, 0, 3), (1, 1, 1, 3), (1, 1, 2, 3), (1, 2, 0, 3),),
     52: ((1, 2, 1, 3), (1, 2, 2, 3), (1, 1, 0, 4), (1, 1, 1, 4), (1, 1, 2, 4), (1, 2, 0, 4), (1, 2, 1, 4), (1, 2, 2, 4),),
 }
@@ -86,9 +87,9 @@
 
 
 def kernel(
-    n, x_hbm, dy_hbm, gate_hbm, up_hbm, down_hbm, dx_hbm, dgate_hbm, dup_hbm, ddown_hbm, h_hbm, gu_hbm,
-    a1, y, g, w, acc, act0, act1, g0, g1, terms, slots, fin, io,
-    sem, io_sem, gu_sem, out_sem, ag_recv, ag_send, side_recv, rs_recv, rs_send, credit,
+    n, x_hbm, dy_hbm, gate_hbm, up_hbm, down_hbm, y, fin, dgate_hbm, dup_hbm, ddown_hbm, h_hbm, gu_hbm,
+    a1, g, w, acc, act0, act1, g0, g1, terms, slots, io,
+    sem, io_sem, gu_sem, first_sem, out_sem, ag_recv, ag_send, side_recv, rs_recv, rs_send, credit,
 ):
     layers, chunks = w.shape[:2]
     tokens, d = y.shape
@@ -157,11 +158,11 @@
                 finish(turn, p, u, far)
 
     def down_out(l, p):
-        return pltpu.make_async_copy(fin.at[p, 2], ddown_hbm.at[l, pl.ds(p * own, own), :], out_sem.at[p])
+        return pltpu.make_async_copy(fin.at[p, 2], ddown_hbm.at[l - 1, pl.ds(p * own, own), :], out_sem.at[p])
 
     def in_out(l, m, j):
         out = dgate_hbm if m == 0 else dup_hbm
-        return pltpu.make_async_copy(fin.at[j, m], out.at[l, :, pl.ds(j * d, d)], out_sem.at[chunks + m * chunks + j])
+        return pltpu.make_async_copy(fin.at[j, m], out.at[l - 1, :, pl.ds(j * d, d)], out_sem.at[chunks + m * chunks + j])
 
     def finish(turn, p, u, far):
         l = layers - 1 - turn
@@ -177,7 +178,7 @@
         if l:
             pl.semaphore_signal(credit.at[0, p, u], 1, device_id=left, device_id_type=pl.DeviceIdType.MESH)
             pl.semaphore_signal(credit.at[1, p, u], 1, device_id=right, device_id_type=pl.DeviceIdType.MESH)
-        if u == 2:
+        if u == 2 and l:
             down_out(l, p).start()
         if u < 2 and p == chunks - 1:
             low = lax.broadcasted_iota(jnp.int32, (own, 128), 1) < 64
@@ -188,7 +189,7 @@
                 for k, (lo, hi) in enumerate(((c0, c1), (c2, c0), (c1, c2))):
                     j, at = divmod(3 * e + k, d // 128)
                     fin[j, u, :, pl.ds(128 * at, 128)] = jnp.where(low, lo, hi).astype(BF)
-            for j in range(3):
+            for j in range(3) if l else ():
                 in_out(l, u, j).start()
 
     shards = (gate_hbm, up_hbm)
@@ -299,11 +300,9 @@
             rows = aligned(i % TILES * tm, tm)
             acc[2] += dot_tn(acts[slot][...], y[rows, :])
 
-        def in_grads(i, slot):
+        def in_grad(i, slot, m):
             rows = aligned(i % TILES * tm, tm)
-            at = a[rows, :]
-            acc[0] += dot_tn(at, gs[slot][:, :fc])
-            acc[1] += dot_tn(at, gs[slot][:, fc:])
+            acc[m] += dot_tn(a[rows, :], gs[slot][:, m * fc : (m + 1) * fc])
 
         def first_of(j):
             return jnp.minimum(2 * j + 1, tiles - 2)
@@ -315,14 +314,17 @@
         io_in(src, 0).start()
         io_in(src, 1).start()
         if turn:
-            for copy in first_tile:
+            block_in(1).start()
+            for copy in first_tiles:
                 copy.wait()
-            block_in(0).start()
-            block_in(1).start()
+            for k in range(2):
+                for m in range(2):
+                    gate_up[0, k, m] = acc[1 + k, pl.ds(m * tm, tm), :]
         for f in (0, half):
-            grads_in(0, 0, f, acc.at[0, pl.ds(0, 2 * tm), :].reshape(2, tm, fc) if turn else None)
+            grads_in(0, 0, f, acc.at[0].reshape(2, tm, fc) if turn else None)
         if turn:
-            acc[0] = jnp.zeros_like(acc[0])
+            for m in range(3):
+                acc[m] = jnp.zeros_like(acc[m])
 
         def body(j, _):
             if not turn:
@@ -330,16 +332,21 @@
                 choose(j, {bodies * c - 1: 3 * chunks - 2 + c for c in range(1, chunks)}, lambda i: arrived(i))
             choose(j, {at: steps for at, steps in table.items() if at < loop}, reduce)
             if turn:
-                block_in(j).wait()
+                pl.when(j > 0)(lambda: block_in(j).wait())
                 pl.when(j + 2 < loop)(lambda: block_in(j + 2).start())
             for k in range(width):
                 i = width * j + k
                 ahead = jnp.minimum(i + 1, tiles - 1)
                 kept = gate_up.at[j % 3, ahead - first_of(j) if k == 0 else 1] if turn else None
-                grads_in(ahead, (k + 1) % 2, 0, kept)
-                down_grad(i, k % 2)
-                grads_in(ahead, (k + 1) % 2, half, kept)
-                in_grads(i, k % 2)
+                parts = [
+                    functools.partial(grads_in, ahead, (k + 1) % 2, 0, kept),
+                    functools.partial(down_grad, i, k % 2),
+                    functools.partial(in_grad, i, k % 2, 0),
+                    functools.partial(grads_in, ahead, (k + 1) % 2, half, kept),
+                    functools.partial(in_grad, i, k % 2, 1),
+                ]
+                for part in ORDERS[turn]:
+                    parts[part]()
             return 0
 
         def chunk(c, _):
@@ -352,7 +359,7 @@
         lax.fori_loop(0, chunks, chunk, 0)
         for copy in pending:
             copy.wait()
-        for copy in first_tile if not turn else ():
+        for copy in first_tiles if not turn else ():
             copy.start()
 
         def inputs(j, _):
@@ -368,16 +375,13 @@
                 dh = (da * scale - wide * along).astype(BF).astype(F32)
                 y[rows, :] = (y[rows, :].astype(F32) + dh).astype(BF)
             pl.when(j + 2 < BODIES)(lambda: io_in(src, j + 2).start())
-            if l == 0:
-                rows = aligned(j * big, big)
-                pltpu.make_async_copy(y.at[rows, :], dx_hbm.at[rows, :], sem.at[0]).start()
             return 0
 
         lax.fori_loop(0, BODIES, inputs, 0)
 
     for m in range(3):
         acc[m] = jnp.zeros_like(acc[m])
-    first_tile = [pltpu.make_async_copy(gu_hbm.at[0, m], acc.at[0, pl.ds(m * tm, tm), :], gu_sem.at[m]) for m in range(2)]
+    first_tiles = [pltpu.make_async_copy(gu_hbm.at[k, m], acc.at[k, pl.ds(m * tm, tm), :], first_sem.at[k, m]) for k in range(3) for m in range(2)]
 
     def with_last(a2, out):
         def io_out(j):
@@ -388,10 +392,10 @@
             pl.when(j == 0)(lambda: arrived(2 * chunks))
             io_in(x_hbm, j).wait()
             pl.when(j >= 2)(lambda: io_out(j - 2).wait())
-            for k in range(2):
-                rows = aligned(j * big + k * tm, tm)
+            for k in range(4):
+                rows = aligned(j * big + k * (tm // 2), tm // 2)
                 hidden = sum(dot(g[c, rows, :fc], w[0, c, 2]) for c in range(chunks))
-                here = pl.ds(k * tm, tm)
+                here = pl.ds(k * (tm // 2), tm // 2)
                 h = (io[j % 2, here, :].astype(F32) + hidden.astype(BF).astype(F32)).astype(BF)
                 out[j % 2, here, :] = h
                 a2[rows, :] = normed(h.astype(F32))
@@ -412,12 +416,6 @@
     pl.run_scoped(with_first, pltpu.VMEM((3, 2, 2, tm, fc), F32))
 
     reduce(SUMS[max(SUMS)])
-    for p in range(chunks):
-        down_out(0, p).wait()
-    for m in range(2):
-        for j in range(3):
-            in_out(0, m, j).wait()
-    pltpu.make_async_copy(y, dx_hbm, sem.at[0]).wait()
     for i in range(len(ITEMS)):
         ref = piece(i, pl.ds(0, (n - 1) * own))
         pltpu.make_async_copy(ref, ref, ag_send.at[i]).wait()
@@ -431,16 +429,21 @@
     items = 3 * CHUNKS + 1
     assert d == fc == n * own and down.shape == (layers, CHUNKS * own, d) and own == 64
     assert n == 8 and layers == 2
-    hbm = pl.BlockSpec(memory_space=pl.ANY)
+    hbm, vmem = pl.BlockSpec(memory_space=pl.ANY), pl.BlockSpec(memory_space=pltpu.VMEM)
     dma = pltpu.SemaphoreType.DMA
     kept = jax.ShapeDtypeStruct((CHUNKS * TILES, 2, tm, fc), F32)
     return pl.pallas_call(
         functools.partial(kernel, n),
-        out_shape=[*(jax.ShapeDtypeStruct(t.shape, BF) for t in (x, gate, up, down, x)), kept],
+        out_shape=[
+            pltpu.VMEM((tokens, d), BF),
+            pltpu.VMEM((CHUNKS, 3, own, fc), BF),
+            *(jax.ShapeDtypeStruct((layers - 1, *t.shape[1:]), BF) for t in (gate, up, down)),
+            jax.ShapeDtypeStruct(x.shape, BF),
+            kept,
+        ],
         in_specs=[hbm] * 5,
-        out_specs=[hbm] * 6,
+        out_specs=[vmem] * 2 + [hbm] * 5,
         scratch_shapes=[
-            pltpu.VMEM((tokens, d), BF),
             pltpu.VMEM((tokens, d), BF),
             pltpu.VMEM((CHUNKS, tokens, 2 * fc), BF),
             pltpu.VMEM((layers, CHUNKS, 3, d, fc), BF),
@@ -451,11 +454,11 @@
             pltpu.VMEM((tm, 2 * fc), BF),
             pltpu.VMEM((CHUNKS, 3, d, fc), BF),
             pltpu.VMEM((CHUNKS, 3, n - 1, own, fc), BF),
-            pltpu.VMEM((CHUNKS, 3, own, fc), BF),
             pltpu.VMEM((2, 2 * tm, d), BF),
             dma((2 + layers * 9,)),
             dma((2, 2)),
             dma((3,)),
+            dma((3, 2)),
             dma((CHUNKS * 3,)),
             dma((items, n - 1)),
             dma((items,)),
@@ -464,43 +467,45 @@
             dma((CHUNKS, 3)),
             pltpu.SemaphoreType.REGULAR((2, CHUNKS, 3)),
         ],
-        compiler_params=pltpu.CompilerParams(vmem_limit_bytes=VMEM_LIMIT, has_side_effects=True, collective_id=0),
+        compiler_params=pltpu.CompilerParams(vmem_limit_bytes=VMEM_LIMIT - (tokens * d + CHUNKS * 3 * own * fc) * 2, has_side_effects=True, collective_id=0),
         name="layers",
-    )(x, dy, gate, up, down)[:4]
-
-
-def copied(*arrays):
-    parts = [t.reshape(-1, t.shape[-1]) for t in arrays]
-    cuts = [8, *(1 for _ in parts[1:])]
-
-    def kernel(*refs):
-        k = len(parts)
-        src, dst, bufs, sems = refs[:k], refs[k : 2 * k], refs[2 * k : 3 * k], refs[3 * k]
-        moves = []
-        for which, (s, t, buf, cut) in enumerate(zip(src, dst, bufs, cuts)):
-            size = s.shape[0] // cut
-            for j in range(cut):
-                rows = pl.ds(j * size, size)
-                at = sems.at[:, 8 * which + j]
-                moves.append((pltpu.make_async_copy(s.at[rows], buf.at[rows], at.at[0]), pltpu.make_async_copy(buf.at[rows], t.at[rows], at.at[1])))
-        for there, _ in moves:
-            there.start()
-        for there, back in moves:
-            there.wait()
-            back.start()
-        for _, back in moves:
-            back.wait()
-
-    hbm = pl.BlockSpec(memory_space=pl.ANY)
-    out = pl.pallas_call(
+    )(x, dy, gate, up, down)[:5]
+
+
+def outputs(layers, dx, first, *others):
+    tokens, d = dx.shape
+    chunks, _, own, fc = first.shape
+    wide, tall = (layers, own, chunks * fc), (layers, chunks * own, d)
+
+    def kernel(dx_ref, first_ref, gate_in, up_in, down_in, dx_out, gate_out, up_out, down_out, *rest):
+        *bufs, sem, in_sem = rest
+        grads = (gate_out, up_out, down_out)
+        ins = [pltpu.make_async_copy(s, buf, in_sem.at[k]) for k, (s, buf) in enumerate(zip((gate_in, up_in, down_in), bufs))]
+        moves = [pltpu.make_async_copy(dx_ref, dx_out, sem.at[0])]
+        for m, out in enumerate(grads):
+            for j in range(chunks):
+                place = out.at[0, :, pl.ds(j * fc, fc)] if m < 2 else out.at[0, pl.ds(j * own, own), :]
+                moves.append(pltpu.make_async_copy(first_ref.at[j, m], place, sem.at[1 + m * chunks + j]))
+        for copy in (*ins, *moves):
+            copy.start()
+        for k, (copy, buf, out) in enumerate(zip(ins, bufs, grads)):
+            copy.wait()
+            moves.append(pltpu.make_async_copy(buf, out.at[pl.ds(1, layers - 1)], sem.at[1 + 3 * chunks + k]))
+            moves[-1].start()
+        for copy in moves:
+            copy.wait()
+
+    hbm, vmem = pl.BlockSpec(memory_space=pl.ANY), pl.BlockSpec(memory_space=pltpu.VMEM)
+    kept = [pltpu.with_memory_space_constraint(t, pltpu.VMEM) for t in (dx, first)]
+    return pl.pallas_call(
         kernel,
-        out_shape=[jax.ShapeDtypeStruct(t.shape, t.dtype) for t in parts],
-        in_specs=[hbm] * len(parts),
-        out_specs=[hbm] * len(parts),
-        scratch_shapes=[*(pltpu.VMEM(t.shape, t.dtype) for t in parts), pltpu.SemaphoreType.DMA((2, 8 * len(parts)))],
+        out_shape=[jax.ShapeDtypeStruct(s, BF) for s in ((tokens, d), wide, wide, tall)],
+        in_specs=[vmem] * 2 + [hbm] * 3,
+        out_specs=[hbm] * 4,
+        scratch_shapes=[*(pltpu.VMEM(t.shape, BF) for t in others), pltpu.SemaphoreType.DMA((4 + 3 * chunks,)), pltpu.SemaphoreType.DMA((3,))],
+        compiler_params=pltpu.CompilerParams(vmem_limit_bytes=VMEM_LIMIT - (dx.size + first.size) * 2),
         name="outputs",
-    )(*parts)
-    return [t.reshape(like.shape) for t, like in zip(out, arrays)]
+    )(*kept, *others)
 
 
 def solution(mesh):
@@ -508,7 +513,7 @@
     assert mesh.shape["rep"] % 2 == 0
 
     def local(x, dy, gate, up, down):
-        dx, *grads = copied(*layers_of(n, x[0], dy[0], gate, up, down))
+        dx, *grads = outputs(gate.shape[0], *layers_of(n, x[0], dy[0], gate, up, down))
         return dx[None], *grads
 
     both, rows = P(("rep", "dp"), None, None), P(None, "dp", None)

time: 193 us -> 186 us (0.964)
  Pallas kernels: 192 us -> 185 us
    pallas_call x2, Pallas kernels: 192 us -> 185 us  [the longest x1 183 us: layers_of(): pl.pallas_call(functools.partial(kernel, n), out_shape=[pltpu.VMEM((token...]
where the time goes in v6:
time: 186 us
  Pallas kernels  185 us (99%)
    pallas_call x1, Pallas kernels, layers_of(): pl.pallas_call(functools.partial(kernel, n), out_shape=[pltpu.VMEM((token...  183 us

profile of v6, /device:TPU:22, one launch (start us, length us, event | category | flops | bytes accessed | tf_op | source)
XLA Modules:
  0.0 186.2 jit_solution(2176579450216284749)
XLA Ops:
  0.6 182.7 %layers.1 = (bf16[4096,512]{1,0:T(8,128)(2,1)S(1)}, bf16[3,3,64,512]{3,2,1,0:T(8,128)(2,1)S(1)}, bf16[1,64,1536]{2,1,0:T(8,128)(2,1)}, bf16[1,64,1536]{2,1,0:T(8...) custom-call(bf16[4096,512]{1,0:T(8,128)(2,1)} %bitcast.3, ...), custom_call_target="tpu_custom_call" | custom-call | tf_op jit(solution)/shard_map/layers/pallas_call | solution.py:435
  183.4 2.6 %outputs.1 = (bf16[4096,512]{1,0:T(8,128)(2,1)}, bf16[2,64,1536]{2,1,0:T(8,128)(2,1)}, bf16[2,64,1536]{2,1,0:T(8,128)(2,1)}, bf16[2,192,512]{2,1,0:T(8,128)(2,1)}) custom-call(bf16[4096,512]{1,0:T(8,128)(2,1)S(1)} %get-tuple-element.13.dx_ref, bf16[3,3,64,512]{3,2,1,0:T(8,128)(2,1)S(1)} %get-tuple-element.14.first_ref, ...), custom_call_target="tpu_custom_call" | custom-call | tf_op jit(solution)/shard_map/outputs/pallas_call | solution.py:500
